TPU v7x, 128 devices: a whole 4x4x4 slice. The times are simulated.
128 devices in a mesh: rep: 1, r: 16 (over y, z), s: 8 (over x, core).
Axes of the slice: x: 4, y: 4, z: 4, core: 2. Of those that a mesh axis runs over, the one named last changes fastest.
Arguments:
- x: bfloat16 [128, 2048, 1152], P(('rep', 'r', 's'))
- dy: bfloat16 [128, 2048, 1152], P(('rep', 'r', 's'))
- w_gate: bfloat16 [2, 1152, 4608], P(None, 's')
- w_up: bfloat16 [2, 1152, 4608], P(None, 's')
- w_down: bfloat16 [2, 4608, 1152], P(None, 's')
Outputs:
- output 1: bfloat16 [128, 2048, 1152], P(('rep', 'r', 's'))
- output 2: bfloat16 [2, 1152, 4608], P('rep', 's')
- output 3: bfloat16 [2, 1152, 4608], P('rep', 's')
- output 4: bfloat16 [2, 4608, 1152], P('rep', 's')
All inputs are finite; a program needn't handle non-finite values.
Results may differ from a plain program's by a relative error of at most 0.018.
Values are sent between devices in bfloat16 or wider.
A program may use at most 1.5 GiB of HBM per device.

v0:
```python
import jax
import jax.numpy as jnp
from jax import lax
from jax.sharding import PartitionSpec as P

NAMES = ("w_gate", "w_up", "w_down")


def matmul(a, w):
    return jnp.dot(a, w, preferred_element_type=jnp.float32).astype(jnp.bfloat16)


def normed(h):
    wide = h.astype(jnp.float32)
    scale = lax.rsqrt(jnp.mean(wide**2, -1, keepdims=True) + 1e-6)
    return (wide * scale).astype(jnp.bfloat16)


def layer(h, w):
    a = normed(h)
    gate = jnp.dot(a, w["w_gate"], preferred_element_type=jnp.float32)
    up = jnp.dot(a, w["w_up"], preferred_element_type=jnp.float32)
    return h + matmul((jax.nn.silu(gate) * up).astype(jnp.bfloat16), w["w_down"])


def solution(mesh):
    def fetched(weights, number):
        return {name: lax.all_gather(w[number], "s", axis=0, tiled=True) for name, w in zip(NAMES, weights, strict=True)}

    def summed(term):
        return lax.psum(lax.psum_scatter(term, "s", scatter_dimension=0, tiled=True), "r")

    def step(x, dy, *weights):
        layers = weights[0].shape[0]
        h, inputs = x[0], []
        for number in range(layers):
            inputs.append(h)
            h = layer(h, fetched(weights, number))
        by_h, mine = dy[0], [None] * layers
        for number in reversed(range(layers)):
            _, back = jax.vjp(lambda w, h: layer(h, w), fetched(weights, number), inputs[number])
            by_w, by_h = back(by_h)
            mine[number] = [summed(by_w[name]) for name in NAMES]
        return (by_h[None], *(jnp.stack([mine[number][i] for number in range(layers)]) for i in range(3)))

    states, cut = P(("rep", "r", "s"), None, None), P(None, "s", None)
    return jax.shard_map(
        step,
        mesh=mesh,
        in_specs=(states, states) + (cut,) * 3,
        out_specs=(states,) + (P("rep", "s", None),) * 3,
        check_vma=False,
    )
```

profile of v0, /device:TPU:0, one launch (start us, length us, event | category | flops | bytes accessed | tf_op | source)
XLA Modules:
  0.0 1086.2 jit_solution(16036035701120095688)
XLA Ops:
  35.1 37.3 %all-gather.13.cloned.1.call-done = bf16[1,1152,4608]{2,1,0:T(8,128)(2,1)} async-done(((bf16[1,144,4608]{2,1,0:T(8,128)(2,1)}), bf16[1,1152,4608]{2,1,0:T(8,128)(2,1)}) %all-gather.13.cloned.1.call-update) | async-done | bytes 10616848 | tf_op jit(solution)/shard_map/all_gather | solution.py:28
  72.4 32.1 %fusion.28 = f32[2048,4608]{1,0:T(8,128)} fusion(bf16[1,1152,4608]{2,1,0:T(8,128)(2,1)} %all-gather.13.cloned.1.call-done, bf16[1,2048,1152]{1,2,0:T(8,128)(2,1)} %copy.10, f32[2048]{0:T(1024)S(1)} %fusion.77), kind=kOutput, calls=%fused_computation.54 | convolution fusion | flops 21750349824 | bytes 53092352 | tf_op jit(solution)/shard_map/dot_general | solution.py:21
  104.5 28.9 %all-gather.15.cloned.1.call-done = bf16[1,1152,4608]{2,1,0:T(8,128)(2,1)} async-done(((bf16[1,144,4608]{2,1,0:T(8,128)(2,1)}), bf16[1,1152,4608]{2,1,0:T(8,128)(2,1)}) %all-gather.15.cloned.1.call-update) | async-done | bytes 10616848 | tf_op jit(solution)/shard_map/all_gather | solution.py:28
  133.4 45.9 %multiply_convert_fusion.1 = (bf16[2048,4608]{1,0:T(8,128)(2,1)}, f32[2048,4608]{1,0:T(8,128)}) fusion(f32[2048,4608]{1,0:T(8,128)} %fusion.28, bf16[1,1152,4608]{2,1,0:T(8,128)(2,1)} %all-gather.15.cloned.1.call-done, bf16[1,2048,1152]{1,2,0:T(8,128)(2,1)} %copy.10, f32[2048]{0:T(1024)S(1)} %fusion.77), kind=kOutput, calls=%fused_computation.13 | convolution fusion | flops 21806972928 | bytes 109715456 | tf_op jit(solution)/shard_map/dot_general | solution.py:22
  194.4 30.7 %fusion.37 = (f32[2048]{0:T(1024)S(1)}, bf16[2048,1152]{0,1:T(8,128)(2,1)}) fusion(bf16[2048,4608]{1,0:T(8,128)(2,1)} %get-tuple-element.20, bf16[1,4608,1152]{2,1,0:T(8,128)(2,1)} %all-gather.17.cloned.1.call-done, bf16[1,2048,1152]{1,2,0:T(8,128)(2,1)} %copy.10), kind=kOutput, calls=%fused_computation.63 | convolution fusion | flops 21755066368 | bytes 38936576 | tf_op jit(solution)/shard_map/dot_general | solution.py:10
  225.1 30.1 %all-gather.21.cloned.1.call-done = bf16[1,4608,1152]{2,1,0:T(8,128)(2,1)} async-done(((bf16[1,576,1152]{2,1,0:T(8,128)(2,1)}), bf16[1,4608,1152]{2,1,0:T(8,128)(2,1)}) %all-gather.21.cloned.1.call-update) | async-done | bytes 10616848 | tf_op jit(solution)/shard_map/all_gather | solution.py:28
  255.2 31.7 %convolution_convert_fusion.1 = bf16[2048,4608]{1,0:T(8,128)(2,1)} fusion(bf16[1,4608,1152]{2,1,0:T(8,128)(2,1)} %all-gather.21.cloned.1.call-done, bf16[1,2048,1152]{2,1,0:T(8,128)(2,1)} %param.6), kind=kOutput, calls=%fused_computation.23 | convolution fusion | flops 21752709120 | bytes 34209792 | tf_op jit(solution)/shard_map/transpose(jvp())/dot_general | solution.py:10
  287.0 29.7 %all-gather.23.cloned.1.call-done = bf16[1,1152,4608]{2,1,0:T(8,128)(2,1)} async-done(((bf16[1,144,4608]{2,1,0:T(8,128)(2,1)}), bf16[1,1152,4608]{2,1,0:T(8,128)(2,1)}) %all-gather.23.cloned.1.call-update) | async-done | bytes 10616848 | tf_op jit(solution)/shard_map/all_gather | solution.py:28
  316.7 32.1 %fusion.12 = f32[2048,4608]{1,0:T(8,128)} fusion(bf16[1,1152,4608]{2,1,0:T(8,128)(2,1)} %all-gather.23.cloned.1.call-done, bf16[2048,1152]{0,1:T(8,128)(2,1)} %get-tuple-element.23, f32[2048]{0:T(1024)S(1)} %fusion.78), kind=kOutput, calls=%fused_computation.38 | convolution fusion | flops 21750349824 | bytes 53092352 | tf_op jit(solution)/shard_map/jvp()/dot_general | solution.py:22
  348.7 29.4 %all-gather.19.cloned.1.call-done = bf16[1,1152,4608]{2,1,0:T(8,128)(2,1)} async-done(((bf16[1,144,4608]{2,1,0:T(8,128)(2,1)}), bf16[1,1152,4608]{2,1,0:T(8,128)(2,1)}) %all-gather.19.cloned.1.call-update) | async-done | bytes 10616848 | tf_op jit(solution)/shard_map/all_gather | solution.py:28
  378.1 52.6 %fusion.1 = (bf16[2048,4608]{1,0:T(8,128)(2,1)}, f32[2048,4608]{1,0:T(8,128)}) fusion(f32[2048,4608]{1,0:T(8,128)} %fusion.12, bf16[2048,4608]{1,0:T(8,128)(2,1)} %convolution_convert_fusion.1, bf16[1,1152,4608]{2,1,0:T(8,128)(2,1)} %all-gather.19.cloned.1.call-done, bf16[2048,1152]{0,1:T(8,128)(2,1)} %get-tuple-element.23, f32[2048]{0:T(1024)S(1)} %fusion.78), kind=kOutput, calls=%fused_computation.7 | convolution fusion | flops 21863596032 | bytes 128589824 | tf_op jit(solution)/shard_map/jvp()/dot_general | solution.py:21
  430.7 29.4 %fusion.46 = bf16[2048,1152]{0,1:T(8,128)(2,1)} fusion(bf16[2048,4608]{1,0:T(8,128)(2,1)} %get-tuple-element.24, bf16[1,1152,4608]{2,1,0:T(8,128)(2,1)} %all-gather.19.cloned.1.call-done), kind=kOutput, calls=%fused_computation.68 | convolution fusion | flops 21743271936 | bytes 34209792 | tf_op jit(solution)/shard_map/transpose(jvp())/dot_general | solution.py:21
  460.1 38.2 %fusion.39 = (f32[2048]{0:T(1024)S(1)}, bf16[2048,1152]{0,1:T(8,128)(2,1)}) fusion(bf16[2048,1152]{0,1:T(8,128)(2,1)} %get-tuple-element.23, bf16[2048,1152]{0,1:T(8,128)(2,1)} %fusion.46, bf16[1,1152,4608]{2,1,0:T(8,128)(2,1)} %all-gather.23.cloned.1.call-done, bf16[2048,4608]{1,0:T(8,128)(2,1)} %convolution_convert_fusion.1, ...), kind=kOutput, calls=%fused_computation.65 | convolution fusion | flops 21814048768 | bytes 81403904 | tf_op jit(solution)/shard_map/transpose(jvp())/dot_general | solution.py:22
  509.1 29.7 %convolution_convert_fusion.3 = bf16[4608,1152]{1,0:T(8,128)(2,1)} fusion(bf16[2048,4608]{1,0:T(8,128)(2,1)} %get-tuple-element.20, bf16[2048,1152]{0,1:T(8,128)(2,1)S(1)} %fusion.66), kind=kOutput, calls=%fused_computation.25 | convolution fusion | flops 21748580352 | bytes 34209792 | tf_op jit(solution)/shard_map/transpose(jvp())/dot_general | solution.py:10
  538.8 37.8 %convolution_convert_fusion.2 = bf16[4608,1152]{1,0:T(8,128)(2,1)} fusion(f32[2048,4608]{1,0:T(8,128)} %fusion.12, bf16[1,2048,1152]{2,1,0:T(8,128)(2,1)} %param.6, f32[2048,4608]{1,0:T(8,128)} %get-tuple-element.25), kind=kOutput, calls=%fused_computation.24 | convolution fusion | flops 21805203456 | bytes 90832896 | tf_op jit(solution)/shard_map/transpose(jvp())/dot_general | solution.py:10
  576.8 51.6 %fusion.3 = (bf16[2048,4608]{1,0:T(8,128)(2,1)}, bf16[2048,4608]{1,0:T(8,128)(2,1)}) fusion(f32[2048,4608]{1,0:T(8,128)} %fusion.28, f32[2048,4608]{1,0:T(8,128)} %get-tuple-element.21, bf16[2048,1152]{0,1:T(8,128)(2,1)} %copy-done, bf16[1,4608,1152]{2,1,0:T(8,128)(2,1)} %all-gather.17.cloned.1.call-done), kind=kOutput, calls=%fused_computation.9 | convolution fusion | flops 21865955328 | bytes 128581632 | tf_op jit(solution)/shard_map/transpose(jvp())/dot_general | solution.py:10
  628.4 34.6 %fusion.10 = bf16[1152,4608]{1,0:T(8,128)(2,1)} fusion(bf16[2048,4608]{1,0:T(8,128)(2,1)} %get-tuple-element.29, bf16[1,2048,1152]{1,2,0:T(8,128)(2,1)} %copy.10, f32[2048]{0:T(1024)S(1)} %copy-done.5, f32[2048,4608]{1,0:T(8,128)} %fusion.28), kind=kOutput, calls=%fused_computation.20 | convolution fusion | flops 21812281344 | bytes 71966720 | tf_op jit(solution)/shard_map/transpose(jvp())/dot_general | solution.py:22
  663.7 34.6 %fusion.11 = bf16[1152,4608]{1,0:T(8,128)(2,1)} fusion(bf16[2048,4608]{1,0:T(8,128)(2,1)} %convolution_convert_fusion.1, bf16[2048,1152]{0,1:T(8,128)(2,1)} %get-tuple-element.23, f32[2048]{0:T(1024)S(1)} %copy-done.7, f32[2048,4608]{1,0:T(8,128)} %get-tuple-element.25), kind=kOutput, calls=%fused_computation.21 | convolution fusion | flops 21812281344 | bytes 71966720 | tf_op jit(solution)/shard_map/transpose(jvp())/dot_general | solution.py:22
  727.0 38.8 %convolution_convert_fusion.5 = bf16[1152,4608]{1,0:T(8,128)(2,1)} fusion(bf16[2048,4608]{1,0:T(8,128)(2,1)} %get-tuple-element.28, bf16[1,2048,1152]{1,2,0:T(8,128)(2,1)} %copy.10, f32[2048]{0:T(1024)S(1)} %copy-done.5), kind=kOutput, calls=%fused_computation.27 | convolution fusion | flops 21750349824 | bytes 34217984 | tf_op jit(solution)/shard_map/transpose(jvp())/dot_general | solution.py:21
  765.9 29.4 %fusion.40 = bf16[2048,1152]{0,1:T(8,128)(2,1)} fusion(bf16[2048,4608]{1,0:T(8,128)(2,1)} %get-tuple-element.28, bf16[1,1152,4608]{2,1,0:T(8,128)(2,1)} %all-gather.13.cloned.1.call-done), kind=kOutput, calls=%fused_computation.66 | convolution fusion | flops 21743271936 | bytes 34209792 | tf_op jit(solution)/shard_map/transpose(jvp())/dot_general | solution.py:21
  798.1 65.2 %reduce-scatter.9.cloned.1.call-done = bf16[144,4608]{1,0:T(8,128)(2,1)} async-done(((bf16[1152,4608]{1,0:T(8,128)(2,1)}), bf16[144,4608]{1,0:T(8,128)(2,1)}) %reduce-scatter.9.cloned.1.call-update) | async-done | bytes 1327120 | tf_op jit(solution)/shard_map/reduce_scatter | solution.py:31
  863.3 65.1 %reduce-scatter.7.cloned.1.call-done = bf16[144,4608]{1,0:T(8,128)(2,1)} async-done(((bf16[1152,4608]{1,0:T(8,128)(2,1)}), bf16[144,4608]{1,0:T(8,128)(2,1)}) %reduce-scatter.7.cloned.1.call-update) | async-done | bytes 1327120 | tf_op jit(solution)/shard_map/reduce_scatter | solution.py:31
  928.4 38.4 %fusion.36 = (f32[2048]{0:T(1024)S(1)}, bf16[2048,1152]{0,1:T(8,128)(2,1)}) fusion(bf16[1,2048,1152]{1,2,0:T(8,128)(2,1)} %copy.10, bf16[2048,1152]{0,1:T(8,128)(2,1)} %fusion.40, bf16[1,1152,4608]{2,1,0:T(8,128)(2,1)} %all-gather.15.cloned.1.call-done, bf16[2048,4608]{1,0:T(8,128)(2,1)} %get-tuple-element.29, f32[2048,4608]{1,0:T(8,128)} %fusion.28), kind=kOutput, calls=%fused_computation.62 | convolution fusion | flops 21814048768 | bytes 81403904 | tf_op jit(solution)/shard_map/transpose(jvp())/dot_general | solution.py:22
  984.8 86.9 %all-reduce.3.cloned.1.call-done = (bf16[1,144,4608]{2,1,0:T(8,128)(2,1)}, bf16[1,144,4608]{2,1,0:T(8,128)(2,1)}, bf16[1,144,4608]{2,1,0:T(8,128)(2,1)}, bf16[1,...) async-done(((bf16[1,144,4608]{2,1,0:T(8,128)(2,1)}, bf16[1,144,4608]{2,1,0:T(8,128)(2,1)}, bf16[1,144,4608]{2,1,0:T(8,128)(2,1)}, ...) | async-done | bytes 7962640 | tf_op jit(solution)/shard_map/psum | solution.py:31
  (67 shorter events, 111.8 us)
Async XLA Ops:
  7.2 7.1 copy-start.1
  7.2 65.2 %all-gather.13.cloned.1.call-start = ((), (), s32[]{:S(2)}) async-start(), calls=%async_computation.12 | async-start | bytes 11943936 | tf_op jit(solution)/shard_map/all_gather | solution.py:28
  10.8 122.6 %all-gather.15.cloned.1.call-start = ((), (), s32[]{:S(2)}) async-start(), calls=%async_computation.13 | async-start | bytes 11943936 | tf_op jit(solution)/shard_map/all_gather | solution.py:28
  14.3 180.1 %all-gather.17.cloned.1.call-start = ((), (), s32[]{:S(2)}) async-start(), calls=%async_computation.14 | async-start | bytes 11943936 | tf_op jit(solution)/shard_map/all_gather | solution.py:28
  16.1 239.2 %all-gather.21.cloned.1.call-start = ((), (), s32[]{:S(2)}) async-start(), calls=%async_computation.16 | async-start | bytes 11943936 | tf_op jit(solution)/shard_map/all_gather | solution.py:28
  16.6 300.0 %all-gather.23.cloned.1.call-start = ((), (), s32[]{:S(2)}) async-start(), calls=%async_computation.17 | async-start | bytes 11943936 | tf_op jit(solution)/shard_map/all_gather | solution.py:28
  17.2 360.9 %all-gather.19.cloned.1.call-start = ((), (), s32[]{:S(2)}) async-start(), calls=%async_computation.15 | async-start | bytes 11943936 | tf_op jit(solution)/shard_map/all_gather | solution.py:28
  17.8 777.4 %reduce-scatter.15.cloned.1.call-start = ((), (), s32[]{:S(2)}) async-start(), calls=%async_computation.10 | async-start | bytes 11943936 | tf_op jit(solution)/shard_map/reduce_scatter | solution.py:31
  27.8 0.6 copy-start.2
  28.4 105.0 %copy-start.4 = (f32[2048]{0:T(1024)}, f32[2048]{0:T(1024)S(1)}, u32[]{:S(2)}) copy-start(f32[2048]{0:T(1024)S(1)} %fusion.77) | copy-start | bytes 24580
  225.1 61.9 %copy-start.8 = (f32[2048]{0:T(1024)}, f32[2048]{0:T(1024)S(1)}, u32[]{:S(2)}) copy-start(f32[2048]{0:T(1024)S(1)} %get-tuple-element.22) | copy-start | bytes 24580
  225.1 273.2 %copy-start.6 = (f32[2048]{0:T(1024)}, f32[2048]{0:T(1024)S(1)}, u32[]{:S(2)}) copy-start(f32[2048]{0:T(1024)S(1)} %fusion.78) | copy-start | bytes 24580
  460.1 38.2 %copy-start.9 = (f32[2048]{0:T(1024)S(1)}, f32[2048]{0:T(1024)}, u32[]{:S(2)}) copy-start(f32[2048]{0:T(1024)} %copy-done.8) | copy-start | bytes 24580
  507.0 2.1 copy-start
  538.8 256.5 %reduce-scatter.17.cloned.1.call-start = ((), (), s32[]{:S(2)}) async-start(), calls=%async_computation.11 | async-start | bytes 11943936 | tf_op jit(solution)/shard_map/reduce_scatter | solution.py:31
  576.7 218.6 %reduce-scatter.11.cloned.1.call-start = ((), (), s32[]{:S(2)}) async-start(), calls=%async_computation.8 | async-start | bytes 11943936 | tf_op jit(solution)/shard_map/reduce_scatter | solution.py:31
  576.7 51.6 %copy-start.5 = (f32[2048]{0:T(1024)S(1)}, f32[2048]{0:T(1024)}, u32[]{:S(2)}) copy-start(f32[2048]{0:T(1024)} %copy-done.4) | copy-start | bytes 24580
  663.0 0.7 copy-start.7
  663.0 135.1 %reduce-scatter.13.cloned.1.call-start = ((), (), s32[]{:S(2)}) async-start(), calls=%async_computation.9 | async-start | bytes 11943936 | tf_op jit(solution)/shard_map/reduce_scatter | solution.py:31
  698.3 165.0 %reduce-scatter.9.cloned.1.call-start = ((), (), s32[]{:S(2)}) async-start(), calls=%async_computation.7 | async-start | bytes 11943936 | tf_op jit(solution)/shard_map/reduce_scatter | solution.py:31
  727.0 201.4 %reduce-scatter.7.cloned.1.call-start = ((), (), s32[]{:S(2)}) async-start(), calls=%async_computation.6 | async-start | bytes 11943936 | tf_op jit(solution)/shard_map/reduce_scatter | solution.py:31
  765.8 305.8 %all-reduce.3.cloned.1.call-start = ((), (), s32[]{:S(2)}) async-start(), calls=%async_computation.18 | async-start | bytes 15925248 | tf_op jit(solution)/shard_map/psum | solution.py:31
  928.4 38.5 %copy-start.3 = (f32[2048]{0:T(1024)S(1)}, f32[2048]{0:T(1024)}, u32[]{:S(2)}) copy-start(f32[2048]{0:T(1024)} %copy-done.2) | copy-start | bytes 24580
Sparse Core Ops, SparseCore 0:
  10.9 61.4 all-gather.12
  74.1 59.2 all-gather.14
  135.1 59.2 all-gather.16
  195.9 59.2 all-gather.20
  257.4 59.2 all-gather.22
  318.8 59.2 all-gather.18
  538.9 63.5 reduce-scatter.14
  605.0 62.7 reduce-scatter.16
  670.2 62.7 reduce-scatter.10
  735.3 62.7 reduce-scatter.12
  800.5 62.7 reduce-scatter.8
  865.6 62.7 reduce-scatter.6
  933.4 138.1 all-reduce.2
where the time goes:
time: 1090 us
  matrix products  616 us (57%)
  waiting for transfers between devices  392 us (36%)
  local copies, waits for them, and re-layouts  31.9 us (3%)
  other arithmetic  31.1 us (3%)
  between operations  14.2 us (1%)
    dot_general x6, matrix products, layer(): up = jnp.dot(a, w['w_up'], preferred_element_type=jnp.float32)  224 us
    dot_general x6, matrix products, layer(): gate = jnp.dot(a, w['w_gate'], preferred_element_type=jnp.float32)  211 us
    dot_general x5, matrix products, matmul(): jnp.dot(a, w, preferred_element_type=jnp.float32).astype(jnp.bfloat16)  182 us
    all_gather x6, waiting for transfers between devices, fetched(): lax.all_gather(w[number], 's', axis=0, tiled=True)  170 us
    reduce_scatter x6, waiting for transfers between devices, summed(): lax.psum_scatter(term, 's', scatter_dimension=0, tiled=True)  133 us
    psum x1, waiting for transfers between devices, summed(): lax.psum(lax.psum_scatter(term, 's', scatter_dimension=0, tiled=True), 'r')  86.9 us
    unnamed x23, local copies, waits for them, and re-layouts  23.3 us
  transfers between devices with their start and end apart: 13, of which 10 were waited for; matrix products, arithmetic and copies ran while one was open for 47% of the time, Pallas kernels for 0%

commit v1 on v0

v1 whole, which is shorter than its diff:
```python
import functools

import jax
import jax.numpy as jnp
from jax import lax
from jax.experimental import pallas as pl
from jax.experimental.pallas import tpu as pltpu
from jax.sharding import PartitionSpec as P

RING = 4
BLOCK = 128
CHUNK = RING * BLOCK
BOTH = 2 * CHUNK
HALF = BLOCK // 2
PART = HALF // RING
VMEM_LIMIT = 66_900_000
SIDES = (1, 3)
OTHERS = (1, 2, 3)
ALL = (0, 1, 2, 3)
f32, bf16 = jnp.float32, jnp.bfloat16


def dot(a, b):
    return jnp.dot(a, b, preferred_element_type=f32)


def dot_nt(a, b):
    return lax.dot_general(a, b, (((1,), (1,)), ((), ())), preferred_element_type=f32)


def dot_tn(a, b):
    return lax.dot_general(a, b, (((0,), (0,)), ((), ())), preferred_element_type=f32)


def rows_at(start, size, unit=None):
    return pl.ds(pl.multiple_of(start, size if unit is None else unit), size)


def add_up(*terms):
    total = terms[0].astype(f32)
    for term in terms[1:]:
        total = total + term.astype(f32)
    return total.astype(bf16)


def scale_of(wide):
    return lax.rsqrt(jnp.mean(wide**2, -1, keepdims=True) + 1e-6)


def normed(h):
    wide = h.astype(f32)
    return (wide * scale_of(wide)).astype(bf16)


def on(cond):
    return pl.when(cond)


class Place:
    def __init__(self):
        r, s = lax.axis_index("r"), lax.axis_index("s")
        self.y, self.z, self.x, self.c = r // RING, lax.rem(r, RING), s // 2, lax.rem(s, 2)

    def at(self, dy=0, dz=0, dx=0, dc=0):
        y, z, x = (lax.rem(v + d, RING) for v, d in ((self.y, dy), (self.z, dz), (self.x, dx)))
        return {"r": y * RING + z, "s": x * 2 + lax.rem(self.c + dc, 2)}

    def along(self, first, step, dc=0):
        return self.at(dy=first * step, dz=(1 - first) * step, dc=dc)


def send(src, dst, send_sem, recv_sem, device):
    pltpu.make_async_remote_copy(
        src_ref=src, dst_ref=dst, send_sem=send_sem, recv_sem=recv_sem, device_id=device, device_id_type=pl.DeviceIdType.MESH
    ).start()


def drain(ref, sem):
    pltpu.make_async_copy(ref, ref, sem).wait()


def meet(devices):
    barrier = pltpu.get_barrier_semaphore()
    for device in devices:
        pl.semaphore_signal(barrier, inc=1, device_id=device, device_id_type=pl.DeviceIdType.MESH)
    pl.semaphore_wait(barrier, len(devices))


class Gather:
    def __init__(self, place, chunks, wg, wu, wd, lent, full_gu, full_d, send_sem, recv_sem):
        self.p, self.chunks = place, chunks
        self.few = chunks // 2
        self.many = chunks - self.few
        self.wg, self.wu, self.wd, self.lent, self.gu, self.d = wg, wu, wd, lent, full_gu, full_d
        self.ss, self.rs = send_sem, recv_sem
        self.rows = wg.shape[1]

    def lend(self, sem):
        for l in range(2):
            for i in range(self.few):
                send(self.wd.at[l, pl.ds((2 * i + 1) * HALF, HALF), :], self.lent.at[l, i], sem.at[0], sem.at[1], self.p.at(dc=1))
        for i in range(2):
            drain(self.lent, sem.at[i])

    def with_down(self, n, use):
        l, k = n // self.chunks, lax.rem(n, self.chunks)
        c = self.p.c
        first = c * self.few
        owned = (k >= first) & (k < first + self.many)
        start = 2 * (k - first) * HALF

        @on(owned)
        def _():
            use(self.wd.at[l, rows_at(start, HALF), :])

        @on(jnp.logical_not(owned))
        def _():
            use(self.lent.at[l, k - (1 - c) * self.many])

    def of(self, n):
        k = lax.rem(n, self.chunks)
        first = 1 - lax.rem(n, 2)
        quarter = first * self.p.y + (1 - first) * self.p.z
        return n // self.chunks, k, first, quarter

    def sems(self, step, n):
        return self.ss.at[step, lax.rem(n, 2)], self.rs.at[step, lax.rem(n, 2)]

    def own_columns(self, j, k):
        return rows_at((j * self.chunks + k) * BLOCK, BLOCK)

    def piece(self, which, n, x, quarter, part=None):
        share = 1 if part is None else 2
        offset = 0 if part is None else part
        if which == "d":
            size = PART // share
            start = x * BLOCK + self.p.c * HALF + quarter * PART + offset * size
            return self.d.at[n, rows_at(start, size), :]
        size = self.rows // share
        start = (2 * x + self.p.c) * self.rows + offset * size
        column = quarter * BLOCK + (CHUNK if which == "u" else 0)
        return self.gu.at[n, rows_at(start, size, 8), rows_at(column, BLOCK)]

    def settle(self, step, n, blocks, columns, rows):
        ss, rs = self.sems(step, n)
        for sems in (rs, ss):
            drain(self.gu.at[0, pl.ds(0, blocks * self.rows), pl.ds(0, columns * BLOCK)], sems.at[0])
            drain(self.d.at[0, pl.ds(0, rows), :], sems.at[1])

    def x1_wide(self, n):
        p = self.p
        l, k, _, _ = self.of(n)
        ss, rs = self.sems(0, n)
        for dx in SIDES:
            send(self.wg.at[l, :, self.own_columns(p.y, k)], self.piece("g", n, p.x, p.y), ss.at[0], rs.at[0], p.at(dx=dx))
            send(self.wu.at[l, :, self.own_columns(p.z, k)], self.piece("u", n, p.x, p.z), ss.at[0], rs.at[0], p.at(dx=dx))

    def x1_down(self, n):
        p = self.p
        _, _, _, q = self.of(n)
        ss, rs = self.sems(0, n)

        def use(ref):
            for dx in SIDES:
                send(ref.at[rows_at(q * PART, PART), :], self.piece("d", n, p.x, q), ss.at[1], rs.at[1], p.at(dx=dx))

        self.with_down(n, use)

    def x1(self, n):
        self.x1_wide(n)
        self.x1_down(n)

    def x2(self, n):
        p = self.p
        _, _, _, q = self.of(n)
        self.settle(0, n, 1, 4, 2 * PART)
        ss, rs = self.sems(1, n)
        for part, to in enumerate(SIDES):
            x = lax.rem(p.x + RING - to, RING)
            for which, quarter, i in (("g", p.y, 0), ("u", p.z, 0), ("d", q, 1)):
                ref = self.piece(which, n, x, quarter, part)
                send(ref, ref, ss.at[i], rs.at[i], p.at(dx=to))

    def settle_x2(self, n):
        self.settle(1, n, 1, 2, PART)

    def round(self, n, q, first, step):
        p = self.p
        return (("g", p.y, p.at(dy=step), 0), ("u", p.z, p.at(dz=step), 0), ("d", q, p.along(first, step), 1))

    def yz1(self, n):
        p = self.p
        _, _, first, q = self.of(n)
        ss, rs = self.sems(2, n)
        for step in SIDES:
            for which, quarter, to, i in self.round(n, q, first, step):
                for dx in OTHERS:
                    ref = self.piece(which, n, lax.rem(p.x + dx, RING), quarter)
                    send(ref, ref, ss.at[i], rs.at[i], to)

    def settle_yz1(self, n):
        self.settle(2, n, 3, 4, 6 * PART)

    def yz2(self, n):
        p = self.p
        _, _, first, q = self.of(n)
        ss, rs = self.sems(3, n)
        for part, step in enumerate(SIDES):
            for which, quarter, to, i in self.round(n, q, first, step):
                for dx in OTHERS:
                    ref = self.piece(which, n, lax.rem(p.x + dx, RING), lax.rem(quarter + RING - step, RING), part)
                    send(ref, ref, ss.at[i], rs.at[i], to)

    def settle_yz2(self, n):
        self.settle(3, n, 3, 2, 3 * PART)

    def device_rows(self, x, c):
        return rows_at((2 * x + c) * self.rows, self.rows, 8), rows_at((2 * x + c) * HALF, HALF)

    def own(self, n, gu, d, copy):
        l, k, _, _ = self.of(n)
        gu_rows, d_rows = self.device_rows(self.p.x, self.p.c)
        for j in ALL:
            for i, w in enumerate((self.wg, self.wu)):
                copy(w.at[l, :, self.own_columns(j, k)], gu.at[gu_rows, pl.ds(i * CHUNK + j * BLOCK, BLOCK)], 0)
        self.with_down(n, lambda ref: copy(ref, d.at[d_rows, :], 1))

    def across(self, n):
        p = self.p
        ss, rs = self.sems(4, n)
        to = p.at(dc=1)
        gu, d = self.gu.at[n], self.d.at[n]
        self.own(n, gu, d, lambda src, dst, i: send(src, dst, ss.at[i], rs.at[i], to))
        for dx in OTHERS:
            gu_rows, d_rows = self.device_rows(lax.rem(p.x + dx, RING), p.c)
            send(gu.at[gu_rows, :], gu.at[gu_rows, :], ss.at[0], rs.at[0], to)
            send(d.at[d_rows, :], d.at[d_rows, :], ss.at[1], rs.at[1], to)

    def arrived(self, n):
        self.settle(4, n, 4, 8, 4 * HALF)

    def load(self, n, slot, gu_v, d_v, sem):
        p = self.p
        gu, d = gu_v.at[slot], d_v.at[slot]
        start = lambda src, dst, i: pltpu.make_async_copy(src, dst, sem.at[slot, i]).start()
        self.own(n, gu, d, start)
        spans = [self.device_rows(p.x, 1 - p.c)]
        for dx in OTHERS:
            x = lax.rem(p.x + dx, RING)
            spans.append((rows_at(2 * x * self.rows, 2 * self.rows, 8), rows_at(x * BLOCK, BLOCK)))
        for gu_rows, d_rows in spans:
            start(self.gu.at[n, gu_rows, :], gu.at[gu_rows, :], 0)
            start(self.d.at[n, d_rows, :], d.at[d_rows, :], 1)

    def loaded(self, slot, gu_v, d_v, sem):
        drain(gu_v.at[slot], sem.at[slot, 0])
        drain(d_v.at[slot], sem.at[slot, 1])


def forward_kernel(chunks, x_ref, wg, wu, wd, full_gu, full_d, lent, kept, h_ref, a_ref, x_v, a_v, y_v, gu_v, d_v, kept_v, ss, rs, ld_sem, kept_sem, io_sem, lend_sem):
    p = Place()
    meet([p.at(dc=1)] + [p.at(**{axis: side}) for axis in ("dx", "dy", "dz") for side in SIDES])
    tokens = x_v.shape[0]
    half = tokens // 2
    tile = min(BLOCK, half)
    g = Gather(p, chunks, wg, wu, wd, lent, full_gu, full_d, ss, rs)
    x_copy = pltpu.make_async_copy(x_ref, x_v, io_sem.at[0])
    x_copy.start()
    g.x1_wide(0)
    g.lend(lend_sem)
    g.x1_down(0)
    g.x1(1)
    x_copy.wait()

    @pl.loop(0, tokens // tile)
    def _(i):
        t = rows_at(i * tile, tile)
        a_v[t, :] = normed(x_v[t, :])
        y_v[t, :] = jnp.zeros((tile, y_v.shape[1]), f32)

    g.x2(0)
    g.x2(1)
    g.settle_x2(0)
    g.yz1(0)
    g.settle_x2(1)
    g.yz1(1)
    g.x1(2)
    g.settle_yz1(0)
    g.yz2(0)
    g.x1(3)
    g.x2(2)
    g.settle_yz2(0)
    g.across(0)
    g.settle_yz1(1)
    g.yz2(1)
    g.settle_x2(2)
    g.yz1(2)
    g.x2(3)
    g.arrived(0)
    g.load(0, 0, gu_v, d_v, ld_sem)

    def part(k, i):
        slot = lax.rem(k, 2)
        t = pl.ds(i * half, half)

        @on(k > 0)
        def _():
            drain(kept_v.at[i], kept_sem.at[i])

        kept_v[i] = dot(a_v[t, :], gu_v[slot])
        pltpu.make_async_copy(kept_v.at[i], kept.at[k, t, :], kept_sem.at[i]).start()
        gate, up = kept_v[i, :, :CHUNK], kept_v[i, :, CHUNK:]
        act = (jax.nn.silu(gate) * up).astype(bf16)
        y_v[t, :] += dot(act, d_v[slot])

    @pl.loop(0, chunks)
    def _(k):
        g.settle_yz2(k + 1)
        g.across(k + 1)
        g.settle_yz1(k + 2)
        g.yz2(k + 2)
        g.settle_x2(k + 3)
        g.yz1(k + 3)
        g.x1(k + 4)
        g.loaded(lax.rem(k, 2), gu_v, d_v, ld_sem)
        part(k, 0)
        g.x2(k + 4)
        g.arrived(k + 1)

        @on(k + 1 < chunks)
        def _():
            g.load(k + 1, lax.rem(k + 1, 2), gu_v, d_v, ld_sem)

        part(k, 1)

    @pl.loop(0, tokens // tile)
    def _(i):
        t = rows_at(i * tile, tile)
        h = add_up(x_v[t, :], y_v[t, :].astype(bf16))
        x_v[t, :] = h
        a_v[t, :] = normed(h)

    h_copy = pltpu.make_async_copy(x_v, h_ref, io_sem.at[0])
    a_copy = pltpu.make_async_copy(a_v, a_ref, io_sem.at[1])
    h_copy.start()
    a_copy.start()
    g.settle_yz2(chunks + 1)
    g.settle_yz1(chunks + 2)
    g.settle_x2(chunks + 3)
    for i in range(2):
        drain(kept_v.at[i], kept_sem.at[i])
    h_copy.wait()
    a_copy.wait()


def vmem(*shape, dtype=bf16):
    return pltpu.VMEM(shape, dtype)


def dma(*shape):
    return pltpu.SemaphoreType.DMA(shape)


def call(kernel, number, ins, outs, scratch, aliases):
    any_ = pl.BlockSpec(memory_space=pl.ANY)
    return pl.pallas_call(
        kernel,
        in_specs=[any_] * len(ins),
        out_specs=[any_] * len(outs),
        out_shape=[jax.ShapeDtypeStruct(shape, dtype) for shape, dtype in outs],
        input_output_aliases=aliases,
        scratch_shapes=scratch,
        compiler_params=pltpu.CompilerParams(collective_id=number, has_side_effects=True, vmem_limit_bytes=VMEM_LIMIT),
    )(*ins)


def forward(x, wg, wu, wd, chunks):
    tokens, d = x.shape
    layers = wg.shape[0]
    n = layers * chunks
    outs = [
        ((n, d, BOTH), bf16),
        ((n, CHUNK, d), bf16),
        ((layers, chunks // 2, HALF, d), bf16),
        ((chunks, tokens, BOTH), f32),
        (x.shape, bf16),
        (x.shape, bf16),
    ]
    scratch = [vmem(tokens, d)] * 2 + [vmem(tokens, d, dtype=f32)]
    scratch += [vmem(2, d, BOTH), vmem(2, CHUNK, d), vmem(2, tokens // 2, BOTH, dtype=f32)]
    scratch += [dma(5, 2, 2)] * 2 + [dma(2, 2)] + [dma(2)] * 3
    return call(functools.partial(forward_kernel, chunks), 0, (x, wg, wu, wd), outs, scratch, {})


class Reduce:
    def __init__(self, place, chunks, own, out, bufs, sems):
        self.p, self.chunks = place, chunks
        self.own_gu, self.own_d = own
        self.out_g, self.out_u, self.out_d = out
        (self.pair_gu, self.pair_d, self.r1_gu, self.r1_d, self.s1_gu, self.s1_d, self.r2_gu, self.r2_d, self.s2_gu, self.s2_d) = bufs[:10]
        (self.f_gu, self.f_d, self.y_g, self.y_u, self.y_d, self.z_g, self.z_u, self.z_d, self.o_g, self.o_u, self.o_d) = bufs[10:]
        (self.pair_s, self.pair_r, self.s1_s, self.s1_r, self.s2_s, self.s2_r, self.y_s, self.y_r, self.z_s, self.z_r, self.o_s, self.o_r, self.l_sem, self.c_r) = sems
        self.rows = self.f_gu.shape[0]

    @staticmethod
    def scratch(rows, d, chunks):
        pair = [vmem(3, RING, rows, BOTH), vmem(3, RING, HALF, d)]
        r1, s1 = ([vmem(*lead, rows, CHUNK), vmem(*lead, HALF // 2, d)] for lead in ((2, 2), (2,)))
        r2, s2, f = ([vmem(*lead, rows, BOTH), vmem(*lead, HALF, d)] for lead in ((2, 2), (2,), ()))
        y, z, o = ([vmem(*lead, rows, BLOCK)] * 2 + [vmem(*lead, PART, d)] for lead in ((3,), (4,), ()))
        bufs = pair + r1 + s1 + r2 + s2 + f + y + z + o
        sems = [dma(3, 2)] * 2 + [dma(2), dma(2, 2)] * 2 + [dma(3)] * 7 + [dma(2 * chunks)]
        return bufs, sems

    def device_rows(self, x, c):
        return rows_at((2 * x + c) * self.rows, self.rows, 8), rows_at((2 * x + c) * HALF, HALF)

    def pair(self, q):
        p = self.p
        slot, slot3 = lax.rem(q, 2), lax.rem(q, 3)
        to = p.at(dc=1)
        for x in ALL:
            gu_rows, d_rows = self.device_rows(x, 1 - p.c)
            send(self.own_gu.at[slot, gu_rows, :], self.pair_gu.at[slot3, x], self.pair_s.at[slot3, 0], self.pair_r.at[slot3, 0], to)
            send(self.own_d.at[slot, d_rows, :], self.pair_d.at[slot3, x], self.pair_s.at[slot3, 1], self.pair_r.at[slot3, 1], to)

    def terms(self, q, x):
        slot, slot3 = lax.rem(q, 2), lax.rem(q, 3)
        gu_rows, d_rows = self.device_rows(x, self.p.c)
        return (self.own_gu[slot, gu_rows, :], self.pair_gu[slot3, x]), (self.own_d[slot, d_rows, :], self.pair_d[slot3, x])

    def x1(self, q):
        p = self.p
        slot, slot3 = lax.rem(q, 2), lax.rem(q, 3)
        for sem in (self.pair_r, self.pair_s):
            drain(self.pair_gu.at[slot3], sem.at[slot3, 0])
            drain(self.pair_d.at[slot3], sem.at[slot3, 1])
        gu, d = self.terms(q, lax.rem(p.x + 2, RING))
        for i in range(2):
            self.s1_gu[i] = add_up(*(t[:, i * CHUNK : (i + 1) * CHUNK] for t in gu))
            self.s1_d[i] = add_up(*(t[i * HALF // 2 : (i + 1) * HALF // 2] for t in d))
        for i, dx in enumerate(SIDES):
            send(self.s1_gu.at[i], self.r1_gu.at[slot, i], self.s1_s.at[0], self.s1_r.at[slot, 0], p.at(dx=dx))
            send(self.s1_d.at[i], self.r1_d.at[slot, i], self.s1_s.at[1], self.s1_r.at[slot, 1], p.at(dx=dx))

    def x2(self, q):
        p = self.p
        slot = lax.rem(q, 2)
        drain(self.r1_gu.at[slot], self.s1_r.at[slot, 0])
        drain(self.r1_d.at[slot], self.s1_r.at[slot, 1])
        drain(self.s1_gu, self.s1_s.at[0])
        drain(self.s1_d, self.s1_s.at[1])
        for i, dx in enumerate(SIDES):
            gu, d = self.terms(q, lax.rem(p.x + dx, RING))
            for j in range(2):
                columns, rows = slice(j * CHUNK, (j + 1) * CHUNK), slice(j * HALF // 2, (j + 1) * HALF // 2)
                self.s2_gu[i, :, columns] = add_up(*(t[:, columns] for t in gu), *((self.r1_gu[slot, i],) if i == j else ()))
                self.s2_d[i, rows, :] = add_up(*(t[rows] for t in d), *((self.r1_d[slot, i],) if i == j else ()))
        for i, dx in enumerate(SIDES):
            send(self.s2_gu.at[i], self.r2_gu.at[slot, i], self.s2_s.at[0], self.s2_r.at[slot, 0], p.at(dx=dx))
            send(self.s2_d.at[i], self.r2_d.at[slot, i], self.s2_s.at[1], self.s2_r.at[slot, 1], p.at(dx=dx))

    def of(self, q):
        p = self.p
        first = 1 - lax.rem(q, 2)
        return first, first * p.y + (1 - first) * p.z, first * p.z + (1 - first) * p.y

    def mine(self, quarter):
        return rows_at(quarter * BLOCK, BLOCK)

    def yz1(self, q):
        p = self.p
        slot = lax.rem(q, 2)
        drain(self.r2_gu.at[slot], self.s2_r.at[slot, 0])
        drain(self.r2_d.at[slot], self.s2_r.at[slot, 1])
        drain(self.s2_gu, self.s2_s.at[0])
        drain(self.s2_d, self.s2_s.at[1])
        gu, d = self.terms(q, p.x)
        self.f_gu[...] = add_up(*gu, self.r2_gu[slot, 0], self.r2_gu[slot, 1])
        self.f_d[...] = add_up(*d, self.r2_d[slot, 0], self.r2_d[slot, 1])
        first, along, _ = self.of(q)
        for i, step in enumerate(OTHERS):
            y, z, a = (lax.rem(v + step, RING) for v in (p.y, p.z, along))
            send(self.f_gu.at[:, self.mine(y)], self.y_g.at[i], self.y_s.at[0], self.y_r.at[0], p.at(dy=step))
            send(self.f_gu.at[:, self.mine(RING + z)], self.y_u.at[i], self.y_s.at[1], self.y_r.at[1], p.at(dz=step))
            send(self.f_d.at[rows_at(a * PART, PART), :], self.y_d.at[i], self.y_s.at[2], self.y_r.at[2], p.along(first, step))

    def yz2(self, q):
        p = self.p
        came = (self.y_g, self.y_u, self.y_d)
        for i, ref in enumerate(came):
            drain(ref, self.y_r.at[i])
            drain(ref, self.y_s.at[i])
        first, along, over = self.of(q)
        own = (self.f_gu[:, self.mine(p.y)], self.f_gu[:, self.mine(RING + p.z)], self.f_d[rows_at(along * PART, PART), :])
        sums = ((self.z_g, p.z), (self.z_u, p.y), (self.z_d, over))
        for (ref, place), term, more in zip(sums, own, came):
            ref[place] = add_up(term, *(more[i] for i in range(3)))
        for step in OTHERS:
            for i, ((ref, place), to) in enumerate(zip(sums, (p.at(dz=step), p.at(dy=step), p.along(1 - first, step)))):
                send(ref.at[place], ref.at[place], self.z_s.at[i], self.z_r.at[i], to)

    def out(self, q):
        p = self.p
        l, k = 1 - q // self.chunks, lax.rem(q, self.chunks)
        _, along, _ = self.of(q)
        column = lambda j: rows_at((j * self.chunks + k) * BLOCK, BLOCK)
        rows = self.chunks * HALF
        row = k * BLOCK + p.c * HALF + along * PART
        g, u = self.out_g.at[l, :, column(p.y)], self.out_u.at[l, :, column(p.z)]
        return (g, u, self.out_d.at[l, rows_at(lax.rem(row, rows), PART), :]), row // rows == p.c

    def lends(self, q):
        row = lax.rem(q, self.chunks) * BLOCK + (1 - self.p.c) * HALF
        return row // (self.chunks * HALF) == self.p.c

    def yz3(self, q):
        p = self.p
        sums = (self.z_g, self.z_u, self.z_d)
        done = (self.o_g, self.o_u, self.o_d)
        for i, ref in enumerate(sums):
            drain(ref.at[pl.ds(0, 3)], self.z_r.at[i])
            drain(ref.at[pl.ds(0, 3)], self.z_s.at[i])
        for ref, total in zip(sums, done):
            total[...] = add_up(*(ref[i] for i in ALL))
        first, _, _ = self.of(q)
        out, owned = self.out(q)

        def spread(i, to):
            pltpu.make_async_copy(done[i], out[i], self.l_sem.at[i]).start()
            for step in OTHERS:
                send(done[i], out[i], self.o_s.at[i], self.o_r.at[i], to(step))

        spread(0, lambda step: p.at(dy=step))
        spread(1, lambda step: p.at(dz=step))

        @on(owned)
        def _():
            spread(2, lambda step: p.along(first, step))

        @on(jnp.logical_not(owned))
        def _():
            for step in ALL:
                send(done[2], out[2], self.o_s.at[2], self.c_r.at[q], p.along(first, step, dc=1))

    def finish(self, q):
        _, owned = self.out(q)

        def settle(i, ref, total):
            drain(ref, self.o_r.at[i])
            drain(ref, self.o_s.at[i])
            drain(total, self.l_sem.at[i])

        settle(0, self.y_g, self.o_g)
        settle(1, self.y_u, self.o_u)

        @on(owned)
        def _():
            settle(2, self.y_d, self.o_d)

        @on(jnp.logical_not(owned))
        def _():
            drain(self.z_d, self.o_s.at[2])

        @on(self.lends(q))
        def _():
            drain(self.z_d, self.c_r.at[q])


def backward_kernel(chunks, a_ref, dy_ref, h_ref, x_ref, kept, wg, wu, wd, lent, full_gu_in, full_d_in, full_gu, full_d, dx_ref, out_g, out_u, out_d, *scratch):
    a_v, dy_v, da_v, gu_v, d_v, dgu_v, act_v, kept_v, *own = scratch[:10]
    (ss, rs, ld_sem, kept_sem, io_sem), bufs, sems = scratch[10:15], scratch[15:36], scratch[36:]
    p = Place()
    meet([p.at(dc=1)] + [p.at(dx=side) for side in SIDES] + [p.at(**{axis: step}, dc=dc) for axis in ("dy", "dz") for step in OTHERS for dc in range(2)])
    tokens, d = a_v.shape
    half, tile = tokens // 2, tokens // 4
    small = min(BLOCK, tile)
    g = Gather(p, chunks, wg, wu, wd, lent, full_gu, full_d, ss, rs)
    r = Reduce(p, chunks, own, (out_g, out_u, out_d), bufs, sems)
    total = 2 * chunks

    def fetch(ref, i):
        return pltpu.make_async_copy(ref, (a_v, dy_v)[i], io_sem.at[i])

    def number(q):
        return (1 - q // chunks) * chunks + lax.rem(q, chunks)

    def keep(t):
        b = lax.rem(t, 2)
        return pltpu.make_async_copy(kept.at[t // 4, rows_at(lax.rem(t, 4) * tile, tile), :], kept_v.at[b], kept_sem.at[b])

    def through_norm(then):
        @pl.loop(0, tokens // small)
        def _(i):
            t = rows_at(i * small, small)
            wide = a_v[t, :].astype(f32)
            scale = scale_of(wide)
            hat = wide * scale
            da = da_v[t, :].astype(bf16).astype(f32)
            back = scale * (da - hat * jnp.mean(da * hat, -1, keepdims=True))
            dy_v[t, :] = add_up(dy_v[t, :], back.astype(bf16))
            da_v[t, :] = jnp.zeros((small, d), f32)
            then(t)

    def through_gate(t, gate, up, slot):
        dact = dot_nt(dy_v[t, :], d_v[slot]).astype(bf16).astype(f32)
        sig = jax.nn.sigmoid(gate)
        silu = gate * sig
        act_v[t, :] = (silu * up).astype(bf16)
        dgu_v[t, :CHUNK] = (dact * up * (sig * (1 + gate * (1 - sig)))).astype(bf16)
        dgu_v[t, CHUNK:] = (dact * silu).astype(bf16)

    def gate_part(q, slot, i):
        @on(q < chunks)
        def _():
            t = pl.ds(i * half, half)
            gu = dot(a_v[t, :], gu_v[slot])
            through_gate(t, gu[:, :CHUNK], gu[:, CHUNK:], slot)

        @on((q >= chunks) & (q < total))
        def _():
            @pl.loop(0, 2)
            def _(j):
                n = (q - chunks) * 4 + 2 * i + j

                @on(n + 1 < 4 * chunks)
                def _():
                    keep(n + 1).start()

                keep(n).wait()
                t = rows_at((2 * i + j) * tile, tile)
                b = lax.rem(n, 2)
                through_gate(t, kept_v[b, :, :CHUNK], kept_v[b, :, CHUNK:], slot)

    fetch(a_ref, 0).start()
    fetch(dy_ref, 1).start()
    g.load(chunks, 0, gu_v, d_v, ld_sem)

    @pl.loop(0, tokens // small)
    def _(i):
        da_v[rows_at(i * small, small), :] = jnp.zeros((small, d), f32)

    fetch(a_ref, 0).wait()
    fetch(dy_ref, 1).wait()

    @pl.loop(0, total + 3)
    def _(q):
        slot = lax.rem(q, 2)
        busy = q < total
        ahead = chunks + q + 2
        gathers = q + 2 < chunks
        one = (q >= 1) & (q <= total)
        two = (q >= 2) & (q <= total + 1)
        three = q >= 3

        @on(one)
        def _():
            r.x1(q - 1)

        @on(gathers & (q >= 2))
        def _():
            g.x1(ahead)

        @on(q == chunks)
        def _():
            fetch(h_ref, 0).wait()

            def then(t):
                pltpu.make_async_copy(x_ref.at[t, :], a_v.at[t, :], io_sem.at[0]).start()

            through_norm(then)
            fetch(x_ref, 0).wait()

            @pl.loop(0, tokens // small)
            def _(i):
                t = rows_at(i * small, small)
                a_v[t, :] = normed(a_v[t, :])

        @on(q == total)
        def _():
            fetch(x_ref, 0).wait()
            through_norm(lambda t: None)
            pltpu.make_async_copy(dy_v, dx_ref, io_sem.at[0]).start()

        @on(busy)
        def _():
            g.loaded(slot, gu_v, d_v, ld_sem)

        gate_part(q, slot, 0)

        @on(three)
        def _():
            r.yz3(q - 3)

        @on(gathers & (q >= 2))
        def _():
            g.x2(ahead)

        @on((q + 1 < chunks) & (q >= 1))
        def _():
            g.settle_yz2(ahead - 1)

        @on(q + 1 < chunks)
        def _():
            g.across(ahead - 1)

        gate_part(q, slot, 1)

        @on(gathers & (q >= 2))
        def _():
            g.settle_x2(ahead)

        @on(gathers & (q >= 1))
        def _():
            g.yz1(ahead)

        @on(two)
        def _():
            r.yz1(q - 2)

        @on(busy)
        def _():
            own[0][slot] = dot_tn(a_v[...], dgu_v[...]).astype(bf16)

        @on(q == chunks - 1)
        def _():
            fetch(h_ref, 0).start()
            keep(0).start()

        @on(q == total - 1)
        def _():
            fetch(x_ref, 0).start()

        @on(one)
        def _():
            r.x2(q - 1)

        @on(q + 1 < chunks)
        def _():
            g.arrived(ahead - 1)

        @on(q + 1 < total)
        def _():
            g.load(number(q + 1), 1 - slot, gu_v, d_v, ld_sem)

        @on(busy)
        def _():
            own[1][slot] = dot_tn(act_v[...], dy_v[...]).astype(bf16)

        @on(three)
        def _():
            r.finish(q - 3)

        @on(busy)
        def _():
            r.pair(q)

        @on(two)
        def _():
            r.yz2(q - 2)

        @on(gathers & (q >= 1))
        def _():
            g.settle_yz1(ahead)

        @on(gathers)
        def _():
            g.yz2(ahead)

        @on(busy)
        def _():
            @pl.loop(0, 2)
            def _(i):
                t = rows_at(i * half, half)
                da_v[t, :] += dot_nt(dgu_v[t, :], gu_v[slot])

    pltpu.make_async_copy(dy_v, dx_ref, io_sem.at[0]).wait()


def backward(a, dy, h, x, kept, wg, wu, wd, lent, full_gu, full_d, chunks):
    tokens, d = x.shape
    ins = (a, dy, h, x, kept, wg, wu, wd, lent, full_gu, full_d)
    outs = [(v.shape, bf16) for v in (full_gu, full_d, x, wg, wu, wd)]
    weights = [vmem(2, d, BOTH), vmem(2, CHUNK, d)]
    scratch = [vmem(tokens, d)] * 2 + [vmem(tokens, d, dtype=f32)] + weights
    scratch += [vmem(tokens, BOTH), vmem(tokens, CHUNK), vmem(2, tokens // 4, BOTH, dtype=f32)] + weights
    scratch += [dma(5, 2, 2)] * 2 + [dma(2, 2)] + [dma(2)] * 2
    bufs, sems = Reduce.scratch(wg.shape[1], d, chunks)
    aliases = {len(ins) - 2: 0, len(ins) - 1: 1}
    return call(functools.partial(backward_kernel, chunks), 1, ins, outs, scratch + bufs + sems, aliases)


def solution(mesh):
    def step(x, dy, wg, wu, wd):
        chunks = wg.shape[2] // CHUNK
        full_gu, full_d, lent, kept, h, a = forward(x[0], wg, wu, wd, chunks)
        _, _, dx, *out = backward(a, dy[0], h, x[0], kept, wg, wu, wd, lent, full_gu, full_d, chunks)
        return dx[None], *out

    states, cut = P(("rep", "r", "s"), None, None), P(None, "s", None)
    return jax.shard_map(
        step,
        mesh=mesh,
        in_specs=(states, states) + (cut,) * 3,
        out_specs=(states,) + (P("rep", "s", None),) * 3,
        check_vma=False,
    )
```

time: 1090 us -> 616 us (0.57)
  matrix products: 616 us -> 0 us
  Pallas kernels: 0 us -> 602 us
  waiting for transfers between devices: 392 us -> 0 us
  other arithmetic: 31.1 us -> 0 us
  local copies, waits for them, and re-layouts: 31.9 us -> 10.8 us
  between operations: 14.2 us -> 0.66 us
    dot_general x17 -> x0, matrix products: 616 us -> none  [the longest x6 224 us: layer(): up = jnp.dot(a, w['w_up'], preferred_element_type=jnp.float32)]
    pallas_call x0 -> x2, Pallas kernels: none -> 602 us  [call(): pl.pallas_call(kernel, in_specs=[any_] * len(ins), out_specs=[any_] * len...]
    all_gather x6 -> x0, waiting for transfers between devices: 170 us -> none  [fetched(): lax.all_gather(w[number], 's', axis=0, tiled=True)]
    reduce_scatter x6 -> x0, waiting for transfers between devices: 133 us -> none  [summed(): lax.psum_scatter(term, 's', scatter_dimension=0, tiled=True)]
    psum x1 -> x0, waiting for transfers between devices: 86.9 us -> none  [summed(): lax.psum(lax.psum_scatter(term, 's', scatter_dimension=0, tiled=True), 'r')]
    unnamed x23 -> x10, local copies, waits for them, and re-layouts: 23.3 us -> 10.8 us
    broadcast_in_dim x1 -> x0, other arithmetic: 11.3 us -> none  [step(): by_h[None]]
  transfers between devices with their start and end apart: 13 -> 0, of which waited for: 10 -> 0; matrix products, arithmetic and copies ran while one was open for 47% -> 0% of each run, Pallas kernels for 0% -> 0%
where the time goes in v1:
time: 616 us; the launch traced here: 614 us
  Pallas kernels  602 us (98%)
  local copies, waits for them, and re-layouts  10.8 us (2%)
    pallas_call x2, Pallas kernels, call(): pl.pallas_call(kernel, in_specs=[any_] * len(ins), out_specs=[any_] * len...  602 us

profile of v1, /device:TPU:0, one launch (start us, length us, event | category | flops | bytes accessed | tf_op | source)
XLA Modules:
  0.0 613.8 jit_solution(975895580887978746)
XLA Ops:
  0.6 125.6 %shard_map.84 = (bf16[18,1152,1024]{2,1,0:T(8,128)(2,1)}, bf16[18,512,1152]{2,1,0:T(8,128)(2,1)}, bf16[2,4,64,1152]{3,2,1,0:T(8,128)(2,1)}, f32[9,2048,1024]{2,1...) custom-call(bf16[2048,1152]{1,0:T(8,128)(2,1)} %bitcast.3, bf16[2,144,4608]{2,1,0:T(8,128)(2,1)} %wg.3, ...), custom_call_target="tpu_custom_call" | custom-call | tf_op jit(solution)/shard_map/pallas_call | solution.py:366
  126.3 476.8 %shard_map.85 = (bf16[18,1152,1024]{2,1,0:T(8,128)(2,1)}, bf16[18,512,1152]{2,1,0:T(8,128)(2,1)}, bf16[2048,1152]{1,0:T(8,128)(2,1)}, bf16[2,144,4608]{2,1,0:T(8...) custom-call(bf16[2048,1152]{1,0:T(8,128)(2,1)} %get-tuple-element.14, ...), custom_call_target="tpu_custom_call", output_to_operand_aliasing={{0}: (9, {}), {1}: (10, {})} | custom-call | tf_op jit(solution)/shard_map/pallas_call | solution.py:366
  603.1 0.0 copy-start.2
  603.1 5.0 copy.17
  608.1 0.0 copy-done.2
  608.1 0.0 copy-start.1
  608.1 0.0 copy-start
  608.1 1.5 copy.18
  609.6 1.2 copy-done.1
  610.8 1.5 copy.19
  612.3 0.0 copy-done
  612.3 1.5 copy.20
Async XLA Ops:
  603.1 5.0 copy-start.2
  608.1 2.7 copy-start.1
  608.1 4.2 copy-start

commit v2 on v0

v2 whole, which is shorter than its diff:
```python
import functools

import jax
import jax.numpy as jnp
from jax import lax
from jax.experimental import pallas as pl
from jax.experimental.pallas import tpu as pltpu
from jax.sharding import PartitionSpec as P

RING = 4
BLOCK = 128
CHUNK = RING * BLOCK
BOTH = 2 * CHUNK
HALF = BLOCK // 2
PART = HALF // RING
VMEM_LIMIT = 66_900_000
SIDES = (1, 3)
OTHERS = (1, 2, 3)
ALL = (0, 1, 2, 3)
f32, bf16 = jnp.float32, jnp.bfloat16


def dot(a, b):
    return jnp.dot(a, b, preferred_element_type=f32)


def dot_nt(a, b):
    return lax.dot_general(a, b, (((1,), (1,)), ((), ())), preferred_element_type=f32)


def dot_tn(a, b):
    return lax.dot_general(a, b, (((0,), (0,)), ((), ())), preferred_element_type=f32)


def rows_at(start, size, unit=None):
    return pl.ds(pl.multiple_of(start, size if unit is None else unit), size)


def add_up(*terms):
    total = terms[0].astype(f32)
    for term in terms[1:]:
        total = total + term.astype(f32)
    return total.astype(bf16)


def scale_of(wide):
    return lax.rsqrt(jnp.mean(wide**2, -1, keepdims=True) + 1e-6)


def normed(h):
    wide = h.astype(f32)
    return (wide * scale_of(wide)).astype(bf16)


def on(cond):
    return pl.when(cond)


class Place:
    def __init__(self):
        r, s = lax.axis_index("r"), lax.axis_index("s")
        self.y, self.z, self.x, self.c = r // RING, lax.rem(r, RING), s // 2, lax.rem(s, 2)

    def at(self, dy=0, dz=0, dx=0, dc=0):
        y, z, x = (lax.rem(v + d, RING) for v, d in ((self.y, dy), (self.z, dz), (self.x, dx)))
        return {"r": y * RING + z, "s": x * 2 + lax.rem(self.c + dc, 2)}

    def along(self, first, step, dc=0):
        return self.at(dy=first * step, dz=(1 - first) * step, dc=dc)


def send(src, dst, send_sem, recv_sem, device):
    pltpu.make_async_remote_copy(
        src_ref=src, dst_ref=dst, send_sem=send_sem, recv_sem=recv_sem, device_id=device, device_id_type=pl.DeviceIdType.MESH
    ).start()


def drain(ref, sem):
    pltpu.make_async_copy(ref, ref, sem).wait()


def meet(devices):
    barrier = pltpu.get_barrier_semaphore()
    for device in devices:
        pl.semaphore_signal(barrier, inc=1, device_id=device, device_id_type=pl.DeviceIdType.MESH)
    pl.semaphore_wait(barrier, len(devices))


class Gather:
    def __init__(self, place, chunks, wg, wu, wd, lent, full_gu, full_d, send_sem, recv_sem):
        self.p, self.chunks = place, chunks
        self.few = chunks // 2
        self.many = chunks - self.few
        self.wg, self.wu, self.wd, self.lent, self.gu, self.d = wg, wu, wd, lent, full_gu, full_d
        self.ss, self.rs = send_sem, recv_sem
        self.rows = wg.shape[1]

    def lend(self, sem):
        for l in range(2):
            for i in range(self.few):
                send(self.wd.at[l, pl.ds((2 * i + 1) * HALF, HALF), :], self.lent.at[l, i], sem.at[0], sem.at[1], self.p.at(dc=1))

    def settle_lend(self, sem):
        for i in range(2):
            drain(self.lent, sem.at[i])

    def with_down(self, n, use):
        l, k = n // self.chunks, lax.rem(n, self.chunks)
        c = self.p.c
        first = c * self.few
        owned = (k >= first) & (k < first + self.many)
        start = 2 * (k - first) * HALF

        @on(owned)
        def _():
            use(self.wd.at[l, rows_at(start, HALF), :])

        @on(jnp.logical_not(owned))
        def _():
            use(self.lent.at[l, k - (1 - c) * self.many])

    def of(self, n):
        k = lax.rem(n, self.chunks)
        first = self.p.c
        quarter = first * self.p.y + (1 - first) * self.p.z
        return n // self.chunks, k, first, quarter

    def sems(self, step, n):
        return self.ss.at[step, lax.rem(n, 2)], self.rs.at[step, lax.rem(n, 2)]

    def own_columns(self, j, k):
        return rows_at((j * self.chunks + k) * BLOCK, BLOCK)

    def piece(self, which, n, x, quarter, part=None):
        share = 1 if part is None else 2
        offset = 0 if part is None else part
        if which == "d":
            size = PART // share
            start = x * BLOCK + self.p.c * HALF + quarter * PART + offset * size
            return self.d.at[n, rows_at(start, size), :]
        size = self.rows // share
        start = (2 * x + self.p.c) * self.rows + offset * size
        column = quarter * BLOCK + (CHUNK if which == "u" else 0)
        return self.gu.at[n, rows_at(start, size, 8), rows_at(column, BLOCK)]

    def settle(self, step, n, blocks, columns, rows):
        ss, rs = self.sems(step, n)
        for sems in (rs, ss):
            drain(self.gu.at[0, pl.ds(0, blocks * self.rows), pl.ds(0, columns * BLOCK)], sems.at[0])
            drain(self.d.at[0, pl.ds(0, rows), :], sems.at[1])

    def x1_wide(self, n):
        p = self.p
        l, k, _, _ = self.of(n)
        ss, rs = self.sems(0, n)
        for dx in SIDES:
            send(self.wg.at[l, :, self.own_columns(p.y, k)], self.piece("g", n, p.x, p.y), ss.at[0], rs.at[0], p.at(dx=dx))
            send(self.wu.at[l, :, self.own_columns(p.z, k)], self.piece("u", n, p.x, p.z), ss.at[0], rs.at[0], p.at(dx=dx))

    def x1_down(self, n):
        p = self.p
        _, _, _, q = self.of(n)
        ss, rs = self.sems(0, n)

        def use(ref):
            for dx in SIDES:
                send(ref.at[rows_at(q * PART, PART), :], self.piece("d", n, p.x, q), ss.at[1], rs.at[1], p.at(dx=dx))

        self.with_down(n, use)

    def x1(self, n):
        self.x1_wide(n)
        self.x1_down(n)

    def x2(self, n):
        p = self.p
        _, _, _, q = self.of(n)
        self.settle(0, n, 1, 4, 2 * PART)
        ss, rs = self.sems(1, n)
        for part, to in enumerate(SIDES):
            x = lax.rem(p.x + RING - to, RING)
            for which, quarter, i in (("g", p.y, 0), ("u", p.z, 0), ("d", q, 1)):
                ref = self.piece(which, n, x, quarter, part)
                send(ref, ref, ss.at[i], rs.at[i], p.at(dx=to))

    def settle_x2(self, n):
        self.settle(1, n, 1, 2, PART)

    def round(self, n, q, first, step):
        p = self.p
        return (("g", p.y, p.at(dy=step), 0), ("u", p.z, p.at(dz=step), 0), ("d", q, p.along(first, step), 1))

    def yz1(self, n):
        p = self.p
        _, _, first, q = self.of(n)
        ss, rs = self.sems(2, n)
        for step in SIDES:
            for which, quarter, to, i in self.round(n, q, first, step):
                for dx in OTHERS:
                    ref = self.piece(which, n, lax.rem(p.x + dx, RING), quarter)
                    send(ref, ref, ss.at[i], rs.at[i], to)

    def settle_yz1(self, n):
        self.settle(2, n, 3, 4, 6 * PART)

    def yz2(self, n):
        p = self.p
        _, _, first, q = self.of(n)
        ss, rs = self.sems(3, n)
        for part, step in enumerate(SIDES):
            for which, quarter, to, i in self.round(n, q, first, step):
                for dx in OTHERS:
                    ref = self.piece(which, n, lax.rem(p.x + dx, RING), lax.rem(quarter + RING - step, RING), part)
                    send(ref, ref, ss.at[i], rs.at[i], to)

    def settle_yz2(self, n):
        self.settle(3, n, 3, 2, 3 * PART)

    def device_rows(self, x, c):
        return rows_at((2 * x + c) * self.rows, self.rows, 8), rows_at((2 * x + c) * HALF, HALF)

    def own(self, n, gu, d, copy):
        l, k, _, _ = self.of(n)
        gu_rows, d_rows = self.device_rows(self.p.x, self.p.c)
        for j in ALL:
            for i, w in enumerate((self.wg, self.wu)):
                copy(w.at[l, :, self.own_columns(j, k)], gu.at[gu_rows, pl.ds(i * CHUNK + j * BLOCK, BLOCK)], 0)
        self.with_down(n, lambda ref: copy(ref, d.at[d_rows, :], 1))

    def across(self, n):
        p = self.p
        ss, rs = self.sems(4, n)
        to = p.at(dc=1)
        gu, d = self.gu.at[n], self.d.at[n]
        self.own(n, gu, d, lambda src, dst, i: send(src, dst, ss.at[i], rs.at[i], to))
        for dx in OTHERS:
            gu_rows, d_rows = self.device_rows(lax.rem(p.x + dx, RING), p.c)
            send(gu.at[gu_rows, :], gu.at[gu_rows, :], ss.at[0], rs.at[0], to)
            send(d.at[d_rows, :], d.at[d_rows, :], ss.at[1], rs.at[1], to)

    def arrived(self, n):
        self.settle(4, n, 4, 8, 4 * HALF)

    def load(self, n, slot, gu_v, d_v, sem):
        p = self.p
        gu, d = gu_v.at[slot], d_v.at[slot]
        start = lambda src, dst, i: pltpu.make_async_copy(src, dst, sem.at[slot, i]).start()
        self.own(n, gu, d, start)
        spans = [self.device_rows(p.x, 1 - p.c)]
        for dx in OTHERS:
            x = lax.rem(p.x + dx, RING)
            spans.append((rows_at(2 * x * self.rows, 2 * self.rows, 8), rows_at(x * BLOCK, BLOCK)))
        for gu_rows, d_rows in spans:
            start(self.gu.at[n, gu_rows, :], gu.at[gu_rows, :], 0)
            start(self.d.at[n, d_rows, :], d.at[d_rows, :], 1)

    def loaded(self, slot, gu_v, d_v, sem):
        drain(gu_v.at[slot], sem.at[slot, 0])
        drain(d_v.at[slot], sem.at[slot, 1])


def vmem(*shape, dtype=bf16):
    return pltpu.VMEM(shape, dtype)


def dma(*shape):
    return pltpu.SemaphoreType.DMA(shape)


class Reduce:
    def __init__(self, place, chunks, kind, own, out, bufs, sems):
        self.p, self.chunks, self.kind, self.own, self.out = place, chunks, kind, own, out
        self.pair_v, self.r1, self.s1, self.r2, self.s2, self.f, self.y, self.z, self.o = bufs
        self.pair_s, self.pair_r, self.s1_s, self.s1_r, self.s2_s, self.s2_r, self.y_s, self.y_r, self.z_s, self.z_r, self.o_s, self.o_r, self.l_sem, self.c_r = sems
        self.rows = self.f.shape[1]

    @staticmethod
    def scratch(kind, rows, d, chunks):
        block, axis = ([rows, CHUNK], 1) if kind < 2 else ([HALF, d], 0)

        def buf(lead, parts):
            shape = list(block)
            shape[axis] //= parts
            return vmem(*lead, *shape)

        r1, s1, r2, s2 = (buf(lead, parts) for parts in (2, 1) for lead in ((2, 2), (2,)))
        bufs = [buf((3, RING), 1), r1, s1, r2, s2, buf((2,), 1), buf((2, 3), RING), buf((2, RING), RING), buf((2,), RING)]
        sems = [dma(3)] * 2 + [dma(1), dma(2)] * 2 + [dma(2)] * 7 + [dma(2 * chunks)]
        return bufs, sems

    def part(self, i, parts):
        if self.kind < 2:
            return slice(None), rows_at(i * (CHUNK // parts), CHUNK // parts)
        return rows_at(i * (HALF // parts), HALF // parts), slice(None)

    def device_rows(self, x, c):
        return rows_at((2 * x + c) * self.rows, self.rows, PART)

    def pair(self, q):
        p = self.p
        slot, slot3 = lax.rem(q, 2), lax.rem(q, 3)
        for x in ALL:
            send(self.own.at[slot, self.device_rows(x, 1 - p.c), :], self.pair_v.at[slot3, x], self.pair_s.at[slot3], self.pair_r.at[slot3], p.at(dc=1))

    def terms(self, q, x, i, parts):
        rows, columns = self.part(i, parts)
        own = self.own.at[lax.rem(q, 2), self.device_rows(x, self.p.c), :]
        return own[rows, columns], self.pair_v.at[lax.rem(q, 3), x][rows, columns]

    def x1(self, q):
        p = self.p
        slot, slot3 = lax.rem(q, 2), lax.rem(q, 3)
        for sem in (self.pair_r, self.pair_s):
            drain(self.pair_v.at[slot3], sem.at[slot3])
        for i in range(2):
            self.s1[i] = add_up(*self.terms(q, lax.rem(p.x + 2, RING), i, 2))
        for i, dx in enumerate(SIDES):
            send(self.s1.at[i], self.r1.at[slot, i], self.s1_s.at[0], self.s1_r.at[slot], p.at(dx=dx))

    def x2(self, q):
        p = self.p
        slot = lax.rem(q, 2)
        drain(self.r1.at[slot], self.s1_r.at[slot])
        drain(self.s1, self.s1_s.at[0])
        for i, dx in enumerate(SIDES):
            for j in range(2):
                more = (self.r1[slot, i],) if i == j else ()
                self.s2.at[i][self.part(j, 2)] = add_up(*self.terms(q, lax.rem(p.x + dx, RING), j, 2), *more)
            send(self.s2.at[i], self.r2.at[slot, i], self.s2_s.at[0], self.s2_r.at[slot], p.at(dx=dx))

    def of(self, q):
        p = self.p
        first = (1, 0, p.c)[self.kind]
        return first, first * p.y + (1 - first) * p.z, first * p.z + (1 - first) * p.y

    def yz1(self, q):
        p = self.p
        slot = lax.rem(q, 2)
        drain(self.r2.at[slot], self.s2_r.at[slot])
        drain(self.s2, self.s2_s.at[0])
        self.f[slot] = add_up(*self.terms(q, p.x, 0, 1), *(self.r2[slot, i] for i in range(2)))
        first, along, _ = self.of(q)
        for i, step in enumerate(OTHERS):
            src = self.f.at[(slot, *self.part(lax.rem(along + step, RING), RING))]
            send(src, self.y.at[slot, i], self.y_s.at[slot], self.y_r.at[slot], p.along(first, step))

    def yz2(self, q):
        p = self.p
        slot = lax.rem(q, 2)
        for sem in (self.y_r, self.y_s):
            drain(self.y.at[slot], sem.at[slot])
        first, along, over = self.of(q)
        self.z[slot, over] = add_up(self.f.at[slot][self.part(along, RING)], *(self.y[slot, i] for i in range(3)))
        for step in OTHERS:
            send(self.z.at[slot, over], self.z.at[slot, over], self.z_s.at[slot], self.z_r.at[slot], p.along(1 - first, step))

    def place_of(self, q):
        p = self.p
        l, k = 1 - q // self.chunks, lax.rem(q, self.chunks)
        _, along, _ = self.of(q)
        if self.kind < 2:
            return self.out.at[l, :, rows_at((along * self.chunks + k) * BLOCK, BLOCK)], None
        rows = self.chunks * HALF
        row = k * BLOCK + p.c * HALF + along * PART
        return self.out.at[l, rows_at(lax.rem(row, rows), PART), :], row // rows == p.c

    def lends(self, q):
        row = lax.rem(q, self.chunks) * BLOCK + (1 - self.p.c) * HALF
        return row // (self.chunks * HALF) == self.p.c

    def yz3(self, q):
        p = self.p
        slot = lax.rem(q, 2)
        for sem in (self.z_r, self.z_s):
            drain(self.z.at[slot, pl.ds(0, 3)], sem.at[slot])
        self.o[slot] = add_up(*(self.z[slot, i] for i in ALL))
        first, _, _ = self.of(q)
        out, owned = self.place_of(q)

        def spread():
            pltpu.make_async_copy(self.o.at[slot], out, self.l_sem.at[slot]).start()
            for step in OTHERS:
                send(self.o.at[slot], out, self.o_s.at[slot], self.o_r.at[slot], p.along(first, step))

        if owned is None:
            spread()
            return
        on(owned)(spread)

        @on(jnp.logical_not(owned))
        def _():
            for step in ALL:
                send(self.o.at[slot], out, self.o_s.at[slot], self.c_r.at[q], p.along(first, step, dc=1))

    def finish(self, q):
        slot = lax.rem(q, 2)
        _, owned = self.place_of(q)

        def settle():
            for sem in (self.o_r, self.o_s):
                drain(self.y.at[slot], sem.at[slot])
            drain(self.o.at[slot], self.l_sem.at[slot])

        if owned is None:
            settle()
            return
        on(owned)(settle)

        @on(jnp.logical_not(owned))
        def _():
            drain(self.z.at[slot], self.o_s.at[slot])

        @on(self.lends(q))
        def _():
            drain(self.z.at[slot], self.c_r.at[q])


def kernel(chunks, x_ref, dy_ref, wg, wu, wd, full_gu, full_d, lent, kept, h_ref, dx_ref, out_g, out_u, out_d, *scratch):
    a_v, dy_v, da_v, gu_v, d_v, dgu_v, act_v, kept_v, own, (ss, rs, ld_sem, kept_sem, io_sem, lend_sem), reduces = scratch
    p = Place()
    meet([p.at(dc=1)] + [p.at(dx=side) for side in SIDES] + [p.at(**{axis: step}, dc=dc) for axis in ("dy", "dz") for step in OTHERS for dc in range(2)])
    tokens, d = a_v.shape
    half = tokens // 2
    small = min(BLOCK, half)
    g = Gather(p, chunks, wg, wu, wd, lent, full_gu, full_d, ss, rs)
    parts = [Reduce(p, chunks, kind, own[kind], (out_g, out_u, out_d)[kind], *reduces[kind]) for kind in (2, 0, 1)]
    total = 2 * chunks

    def tiles(start, stop, count, use):
        steps = tokens // small

        @pl.loop(start * steps // count, stop * steps // count)
        def _(i):
            use(rows_at(i * small, small))

    x_copy = pltpu.make_async_copy(x_ref, dy_v, io_sem.at[0])
    x_copy.start()
    g.lend(lend_sem)
    g.x1_wide(0)
    x_copy.wait()

    def first_norm(t):
        a_v[t, :] = normed(dy_v[t, :])
        da_v[t, :] = jnp.zeros((small, d), f32)

    tiles(0, 1, 4, first_norm)
    g.settle_lend(lend_sem)
    g.x1_down(0)
    g.x1(1)
    tiles(1, 3, 4, first_norm)
    g.x2(0)
    tiles(3, 4, 4, first_norm)
    g.x2(1)
    g.settle_x2(0)
    g.yz1(0)
    g.settle_x2(1)
    g.yz1(1)
    g.x1(2)
    g.settle_yz1(0)
    g.yz2(0)
    g.x1(3)
    g.x2(2)
    g.settle_yz2(0)
    g.across(0)
    g.settle_yz1(1)
    g.yz2(1)
    g.settle_x2(2)
    g.yz1(2)
    g.x2(3)
    g.arrived(0)
    g.load(0, 0, gu_v, d_v, ld_sem)

    def gather_on(n):
        @on(n + 1 < total)
        def _():
            g.settle_yz2(n + 1)
            g.across(n + 1)

        @on(n + 2 < total)
        def _():
            g.settle_yz1(n + 2)
            g.yz2(n + 2)

        @on(n + 3 < total)
        def _():
            g.settle_x2(n + 3)
            g.yz1(n + 3)

        @on(n + 4 < total)
        def _():
            g.x1(n + 4)

    def gather_more(n):
        @on(n + 4 < total)
        def _():
            g.x2(n + 4)

        @on(n + 1 < total)
        def _():
            g.arrived(n + 1)

    def forward_part(k, i):
        slot = lax.rem(k, 2)
        t = rows_at(i * half, half)

        @on(k > 0)
        def _():
            drain(kept_v.at[i], kept_sem.at[i])

        kept_v[i] = dot(a_v[t, :], gu_v[slot])
        pltpu.make_async_copy(kept_v.at[i], kept.at[k, t, :], kept_sem.at[i]).start()
        gate, up = kept_v[i, :, :CHUNK], kept_v[i, :, CHUNK:]
        act = (jax.nn.silu(gate) * up).astype(bf16)
        da_v[t, :] += dot(act, d_v[slot])

    @pl.loop(0, chunks)
    def _(k):
        gather_on(k)
        g.loaded(lax.rem(k, 2), gu_v, d_v, ld_sem)
        forward_part(k, 0)
        gather_more(k)
        g.load(k + 1, lax.rem(k + 1, 2), gu_v, d_v, ld_sem)
        forward_part(k, 1)

    def between(t):
        h = add_up(dy_v[t, :], da_v[t, :].astype(bf16))
        a_v[t, :] = normed(h)
        da_v[t, :] = jnp.zeros((small, d), f32)
        dgu_v[t, :] = h[:, :BOTH]
        act_v[t, : d - BOTH] = h[:, BOTH:]
        pltpu.make_async_copy(dy_ref.at[t, :], dy_v.at[t, :], io_sem.at[0]).start()
        pltpu.make_async_copy(dgu_v.at[t, :], h_ref.at[t, :BOTH], io_sem.at[1]).start()
        pltpu.make_async_copy(act_v.at[t, : d - BOTH], h_ref.at[t, BOTH:], io_sem.at[1]).start()

    tiles(0, 1, 1, between)
    drain(dy_v, io_sem.at[0])
    drain(a_v, io_sem.at[1])
    for i in range(2):
        drain(kept_v.at[i], kept_sem.at[i])

    def each(step, q):
        for part in parts:
            getattr(part, step)(q)

    def fetch(ref):
        return pltpu.make_async_copy(ref, a_v, io_sem.at[0])

    def number(q):
        return (1 - q // chunks) * chunks + lax.rem(q, chunks)

    def keep(t):
        b = lax.rem(t, 2)
        return pltpu.make_async_copy(kept.at[t // 2, rows_at(b * half, half), :], kept_v.at[b], kept_sem.at[b])

    def through_norm(start, stop, then):
        def use(t):
            wide = a_v[t, :].astype(f32)
            scale = scale_of(wide)
            hat = wide * scale
            da = da_v[t, :].astype(bf16).astype(f32)
            back = scale * (da - hat * jnp.mean(da * hat, -1, keepdims=True))
            dy_v[t, :] = add_up(dy_v[t, :], back.astype(bf16))
            da_v[t, :] = jnp.zeros((small, d), f32)
            then(t)

        tiles(start, stop, 2, use)

    def through_gate(t, gate, up, slot):
        dact = dot_nt(dy_v[t, :], d_v[slot]).astype(bf16).astype(f32)
        sig = jax.nn.sigmoid(gate)
        silu = gate * sig
        act_v[t, :] = (silu * up).astype(bf16)
        dgu_v[t, :CHUNK] = (dact * up * (sig * (1 + gate * (1 - sig)))).astype(bf16)
        dgu_v[t, CHUNK:] = (dact * silu).astype(bf16)

    def da_tile(t, slot):
        da_v[t, :] += dot_nt(dgu_v[t, :], gu_v[slot])

    def gate_part(q, slot, i):
        k = lax.rem(q, chunks)

        def layer1(joined):
            t = rows_at(i * half, half)
            if joined:
                da_tile(t, 1 - slot)
            gu = dot(a_v[t, :], gu_v[slot])
            through_gate(t, gu[:, :CHUNK], gu[:, CHUNK:], slot)

        def layer0(joined):
            n = (q - chunks) * 2 + i
            keep(n).wait()
            t = rows_at(i * half, half)
            if joined:
                da_tile(t, 1 - slot)
            through_gate(t, kept_v[i, :, :CHUNK], kept_v[i, :, CHUNK:], slot)

            @on(n + 2 < 2 * chunks)
            def _():
                keep(n + 2).start()

        for joined in (False, True):
            on((q < chunks) & ((k > 0) == joined))(functools.partial(layer1, joined))
            on((q >= chunks) & (q < total) & ((k > 0) == joined))(functools.partial(layer0, joined))

    @pl.loop(0, total + 4)
    def _(q):
        slot, side = lax.rem(q, 2), lax.rem(q + chunks, 2)
        busy = q < total
        ahead = chunks + q
        one = (q >= 1) & (q <= total)
        two = (q >= 2) & (q <= total + 1)
        three = (q >= 3) & (q <= total + 2)

        @on(q >= 4)
        def _():
            each("finish", q - 4)

        @on(three)
        def _():
            each("yz2", q - 3)

        @on((q == chunks) | (q == total))
        def _():
            @pl.loop(0, 2)
            def _(i):
                da_tile(rows_at(i * half, half), 1 - side)

        @on(q == chunks)
        def _():
            fetch(h_ref).wait()

            def then(t):
                pltpu.make_async_copy(x_ref.at[t, :], a_v.at[t, :], io_sem.at[0]).start()

            through_norm(0, 2, then)
            fetch(x_ref).wait()

            def again(t):
                a_v[t, :] = normed(a_v[t, :])

            tiles(0, 1, 1, again)

        gather_on(ahead)

        @on(busy)
        def _():
            g.loaded(side, gu_v, d_v, ld_sem)

        @pl.loop(0, 2)
        def _(i):
            @on(one & (i == 1))
            def _():
                each("x1", q - 1)

            gate_part(q, side, i)

        @on(three)
        def _():
            each("yz3", q - 3)

        @on(two)
        def _():
            each("yz1", q - 2)

        gather_more(ahead)

        @on(q + 1 < total)
        def _():
            g.load(number(q + 1), 1 - side, gu_v, d_v, ld_sem)

        @on(busy)
        def _():
            own[2][slot] = dot_tn(act_v[...], dy_v[...]).astype(bf16)
            parts[0].pair(q)

        @on(q == total)
        def _():
            fetch(x_ref).wait()
            through_norm(0, 1, lambda t: None)

        @on(one)
        def _():
            each("x2", q - 1)

        @on(busy)
        def _():
            both = dot_tn(a_v[...], dgu_v[...]).astype(bf16)
            own[0][slot] = both[:, :CHUNK]
            own[1][slot] = both[:, CHUNK:]
            for part in parts[1:]:
                part.pair(q)

        @on(q == total)
        def _():
            through_norm(1, 2, lambda t: None)
            pltpu.make_async_copy(dy_v, dx_ref, io_sem.at[0]).start()

        @on(q == chunks - 1)
        def _():
            fetch(h_ref).start()
            keep(0).start()
            keep(1).start()

        @on(q == total - 1)
        def _():
            fetch(x_ref).start()

    pltpu.make_async_copy(dy_v, dx_ref, io_sem.at[0]).wait()


def call(x, dy, wg, wu, wd, chunks):
    tokens, d = x.shape
    layers, rows, _ = wg.shape
    n = layers * chunks
    shapes = [(n, d, BOTH), (n, CHUNK, d), (layers, chunks // 2, HALF, d), (chunks, tokens, BOTH), x.shape, x.shape, wg.shape, wu.shape, wd.shape]
    outs = [jax.ShapeDtypeStruct(shape, f32 if shape == (chunks, tokens, BOTH) else bf16) for shape in shapes]
    scratch = [vmem(tokens, d)] * 2 + [vmem(tokens, d, dtype=f32), vmem(2, d, BOTH), vmem(2, CHUNK, d)]
    scratch += [vmem(tokens, BOTH), vmem(tokens, CHUNK), vmem(2, tokens // 2, BOTH, dtype=f32)]
    scratch += [[vmem(2, d, CHUNK)] * 2 + [vmem(2, CHUNK, d)]]
    scratch += [[dma(5, 2, 2)] * 2 + [dma(2, 2)] + [dma(2)] * 3]
    scratch += [[Reduce.scratch(kind, rows, d, chunks) for kind in range(3)]]
    any_ = pl.BlockSpec(memory_space=pl.ANY)
    ins = (x, dy, wg, wu, wd)
    return pl.pallas_call(
        functools.partial(kernel, chunks),
        in_specs=[any_] * len(ins),
        out_specs=[any_] * len(outs),
        out_shape=outs,
        scratch_shapes=scratch,
        compiler_params=pltpu.CompilerParams(collective_id=0, has_side_effects=True, vmem_limit_bytes=VMEM_LIMIT),
        name="stack",
    )(*ins)


def solution(mesh):
    def step(x, dy, wg, wu, wd):
        dx, *out = call(x[0], dy[0], wg, wu, wd, wg.shape[2] // CHUNK)[5:]
        return dx[None], *out

    states, cut = P(("rep", "r", "s"), None, None), P(None, "s", None)
    return jax.shard_map(
        step,
        mesh=mesh,
        in_specs=(states, states) + (cut,) * 3,
        out_specs=(states,) + (P("rep", "s", None),) * 3,
        check_vma=False,
    )
```

time: 1090 us -> 574 us (0.53)
  matrix products: 616 us -> 0 us
  Pallas kernels: 0 us -> 561 us
  waiting for transfers between devices: 392 us -> 0 us
  other arithmetic: 31.1 us -> 0 us
  local copies, waits for them, and re-layouts: 31.9 us -> 12 us
  between operations: 14.2 us -> 0.65 us
    dot_general x17 -> x0, matrix products: 616 us -> none  [the longest x6 224 us: layer(): up = jnp.dot(a, w['w_up'], preferred_element_type=jnp.float32)]
    pallas_call x0 -> x1, Pallas kernels: none -> 561 us  [call(): pl.pallas_call(functools.partial(kernel, chunks), in_specs=[any_] * len(i...]
    all_gather x6 -> x0, waiting for transfers between devices: 170 us -> none  [fetched(): lax.all_gather(w[number], 's', axis=0, tiled=True)]
    reduce_scatter x6 -> x0, waiting for transfers between devices: 133 us -> none  [summed(): lax.psum_scatter(term, 's', scatter_dimension=0, tiled=True)]
    psum x1 -> x0, waiting for transfers between devices: 86.9 us -> none  [summed(): lax.psum(lax.psum_scatter(term, 's', scatter_dimension=0, tiled=True), 'r')]
    unnamed x23 -> x10, local copies, waits for them, and re-layouts: 23.3 us -> 12 us
    broadcast_in_dim x1 -> x0, other arithmetic: 11.3 us -> none  [step(): by_h[None]]
  transfers between devices with their start and end apart: 13 -> 0, of which waited for: 10 -> 0; matrix products, arithmetic and copies ran while one was open for 47% -> 0% of each run, Pallas kernels for 0% -> 0%
where the time goes in v2:
time: 574 us
  Pallas kernels  561 us (98%)
  local copies, waits for them, and re-layouts  12 us (2%)
    pallas_call x1, Pallas kernels, call(): pl.pallas_call(functools.partial(kernel, chunks), in_specs=[any_] * len(i...  561 us
    unnamed x10, local copies, waits for them, and re-layouts  12 us

profile of v2, /device:TPU:0, one launch (start us, length us, event | category | flops | bytes accessed | tf_op | source)
XLA Modules:
  0.0 573.5 jit_solution(569377605351781802)
XLA Ops:
  0.6 560.9 %stack.1 = (bf16[18,1152,1024]{2,1,0:T(8,128)(2,1)}, bf16[18,512,1152]{2,1,0:T(8,128)(2,1)}, bf16[2,4,64,1152]{3,2,1,0:T(8,128)(2,1)}, f32[9,2048,1024]{2,1,0:T(...) custom-call(bf16[2048,1152]{1,0:T(8,128)(2,1)} %bitcast.4, ...), custom_call_target="tpu_custom_call" | custom-call | tf_op jit(solution)/shard_map/stack/pallas_call | solution.py:724
  561.5 0.0 copy-start.2
  561.6 5.0 copy.13
  566.6 0.0 copy-done.2
  566.6 0.0 copy-start.1
  566.6 1.5 copy.14
  568.1 1.2 copy-done.1
  569.3 0.0 copy-start
  569.3 1.5 copy.15
  570.8 1.2 copy-done
  572.0 1.5 copy.16
Async XLA Ops:
  561.5 5.0 copy-start.2
  566.6 2.7 copy-start.1
  569.3 2.7 copy-start

commit v3 on v2

--- a/solution.py
+++ b/solution.py
@@ -17,6 +17,8 @@
 SIDES = (1, 3)
 OTHERS = (1, 2, 3)
 ALL = (0, 1, 2, 3)
+KINDS = (0, 1)
+WIDE, DOWN = (0,), (1,)
 f32, bf16 = jnp.float32, jnp.bfloat16
 
 
@@ -94,6 +96,7 @@
         self.wg, self.wu, self.wd, self.lent, self.gu, self.d = wg, wu, wd, lent, full_gu, full_d
         self.ss, self.rs = send_sem, recv_sem
         self.rows = wg.shape[1]
+        self.total = wg.shape[0] * chunks
 
     def lend(self, sem):
         for l in range(2):
@@ -131,31 +134,31 @@
     def own_columns(self, j, k):
         return rows_at((j * self.chunks + k) * BLOCK, BLOCK)
 
-    def piece(self, which, n, x, quarter, part=None):
+    def piece(self, which, n, slots, quarter, part=None):
         share = 1 if part is None else 2
         offset = 0 if part is None else part
         if which == "d":
             size = PART // share
-            start = x * BLOCK + self.p.c * HALF + quarter * PART + offset * size
-            return self.d.at[n, rows_at(start, size), :]
+            return self.d.at[n, slots, self.p.c, rows_at(quarter * PART + offset * size, size), :]
         size = self.rows // share
-        start = (2 * x + self.p.c) * self.rows + offset * size
         column = quarter * BLOCK + (CHUNK if which == "u" else 0)
-        return self.gu.at[n, rows_at(start, size, 8), rows_at(column, BLOCK)]
-
-    def settle(self, step, n, blocks, columns, rows):
+        return self.gu.at[n, slots, self.p.c, pl.ds(offset * size, size), rows_at(column, BLOCK)]
+
+    def settle(self, step, n, kinds, blocks, columns, rows):
         ss, rs = self.sems(step, n)
-        for sems in (rs, ss):
-            drain(self.gu.at[0, pl.ds(0, blocks * self.rows), pl.ds(0, columns * BLOCK)], sems.at[0])
-            drain(self.d.at[0, pl.ds(0, rows), :], sems.at[1])
+        refs = self.gu.at[0, pl.ds(0, blocks), 0, :, pl.ds(0, columns * BLOCK)], self.d.at[0, pl.ds(0, blocks), 0, pl.ds(0, rows), :]
+        for i in kinds:
+            for sems in (rs, ss):
+                drain(refs[i], sems.at[i])
 
     def x1_wide(self, n):
         p = self.p
         l, k, _, _ = self.of(n)
         ss, rs = self.sems(0, n)
         for dx in SIDES:
-            send(self.wg.at[l, :, self.own_columns(p.y, k)], self.piece("g", n, p.x, p.y), ss.at[0], rs.at[0], p.at(dx=dx))
-            send(self.wu.at[l, :, self.own_columns(p.z, k)], self.piece("u", n, p.x, p.z), ss.at[0], rs.at[0], p.at(dx=dx))
+            slot = RING - dx
+            send(self.wg.at[l, :, self.own_columns(p.y, k)], self.piece("g", n, slot, p.y), ss.at[0], rs.at[0], p.at(dx=dx))
+            send(self.wu.at[l, :, self.own_columns(p.z, k)], self.piece("u", n, slot, p.z), ss.at[0], rs.at[0], p.at(dx=dx))
 
     def x1_down(self, n):
         p = self.p
@@ -164,7 +167,7 @@
 
         def use(ref):
             for dx in SIDES:
-                send(ref.at[rows_at(q * PART, PART), :], self.piece("d", n, p.x, q), ss.at[1], rs.at[1], p.at(dx=dx))
+                send(ref.at[rows_at(q * PART, PART), :], self.piece("d", n, RING - dx, q), ss.at[1], rs.at[1], p.at(dx=dx))
 
         self.with_down(n, use)
 
@@ -172,91 +175,75 @@
         self.x1_wide(n)
         self.x1_down(n)
 
-    def x2(self, n):
+    def x2(self, n, kinds=KINDS):
         p = self.p
         _, _, _, q = self.of(n)
-        self.settle(0, n, 1, 4, 2 * PART)
+        self.settle(0, n, kinds, 1, 4, 2 * PART)
         ss, rs = self.sems(1, n)
         for part, to in enumerate(SIDES):
-            x = lax.rem(p.x + RING - to, RING)
             for which, quarter, i in (("g", p.y, 0), ("u", p.z, 0), ("d", q, 1)):
-                ref = self.piece(which, n, x, quarter, part)
-                send(ref, ref, ss.at[i], rs.at[i], p.at(dx=to))
-
-    def settle_x2(self, n):
-        self.settle(1, n, 1, 2, PART)
-
-    def round(self, n, q, first, step):
-        p = self.p
-        return (("g", p.y, p.at(dy=step), 0), ("u", p.z, p.at(dz=step), 0), ("d", q, p.along(first, step), 1))
-
-    def yz1(self, n):
+                if i in kinds:
+                    src, dst = (self.piece(which, n, slot, quarter, part) for slot in (RING - to, 2))
+                    send(src, dst, ss.at[i], rs.at[i], p.at(dx=to))
+
+    def round(self, n, kinds, step):
         p = self.p
         _, _, first, q = self.of(n)
+        pieces = (("g", p.y, p.at(dy=step), 0), ("u", p.z, p.at(dz=step), 0), ("d", q, p.along(first, step), 1))
+        return [piece for piece in pieces if piece[-1] in kinds]
+
+    def yz1(self, n, kinds=KINDS):
+        p = self.p
+        self.settle(1, n, kinds, 1, 2, PART)
         ss, rs = self.sems(2, n)
         for step in SIDES:
-            for which, quarter, to, i in self.round(n, q, first, step):
-                for dx in OTHERS:
-                    ref = self.piece(which, n, lax.rem(p.x + dx, RING), quarter)
-                    send(ref, ref, ss.at[i], rs.at[i], to)
-
-    def settle_yz1(self, n):
-        self.settle(2, n, 3, 4, 6 * PART)
-
-    def yz2(self, n):
-        p = self.p
-        _, _, first, q = self.of(n)
+            for which, quarter, to, i in self.round(n, kinds, step):
+                ref = self.piece(which, n, pl.ds(1, 3), quarter)
+                send(ref, ref, ss.at[i], rs.at[i], to)
+
+    def yz2(self, n, kinds=KINDS):
+        p = self.p
+        self.settle(2, n, kinds, 3, 4, 2 * PART)
         ss, rs = self.sems(3, n)
         for part, step in enumerate(SIDES):
-            for which, quarter, to, i in self.round(n, q, first, step):
-                for dx in OTHERS:
-                    ref = self.piece(which, n, lax.rem(p.x + dx, RING), lax.rem(quarter + RING - step, RING), part)
-                    send(ref, ref, ss.at[i], rs.at[i], to)
-
-    def settle_yz2(self, n):
-        self.settle(3, n, 3, 2, 3 * PART)
-
-    def device_rows(self, x, c):
-        return rows_at((2 * x + c) * self.rows, self.rows, 8), rows_at((2 * x + c) * HALF, HALF)
-
-    def own(self, n, gu, d, copy):
+            for which, quarter, to, i in self.round(n, kinds, step):
+                ref = self.piece(which, n, pl.ds(1, 3), lax.rem(quarter + RING - step, RING), part)
+                send(ref, ref, ss.at[i], rs.at[i], to)
+
+    def own(self, n, kinds, places, copy):
         l, k, _, _ = self.of(n)
-        gu_rows, d_rows = self.device_rows(self.p.x, self.p.c)
-        for j in ALL:
-            for i, w in enumerate((self.wg, self.wu)):
-                copy(w.at[l, :, self.own_columns(j, k)], gu.at[gu_rows, pl.ds(i * CHUNK + j * BLOCK, BLOCK)], 0)
-        self.with_down(n, lambda ref: copy(ref, d.at[d_rows, :], 1))
-
-    def across(self, n):
-        p = self.p
+        if 0 in kinds:
+            for j in ALL:
+                for i, w in enumerate((self.wg, self.wu)):
+                    copy(w.at[l, :, self.own_columns(j, k)], places[0].at[:, pl.ds(i * CHUNK + j * BLOCK, BLOCK)], 0)
+        if 1 in kinds:
+            self.with_down(n, lambda ref: copy(ref, places[1], 1))
+
+    def across(self, n, kinds=KINDS):
+        c = self.p.c
+        self.settle(3, n, kinds, 3, 2, PART)
         ss, rs = self.sems(4, n)
-        to = p.at(dc=1)
-        gu, d = self.gu.at[n], self.d.at[n]
-        self.own(n, gu, d, lambda src, dst, i: send(src, dst, ss.at[i], rs.at[i], to))
-        for dx in OTHERS:
-            gu_rows, d_rows = self.device_rows(lax.rem(p.x + dx, RING), p.c)
-            send(gu.at[gu_rows, :], gu.at[gu_rows, :], ss.at[0], rs.at[0], to)
-            send(d.at[d_rows, :], d.at[d_rows, :], ss.at[1], rs.at[1], to)
-
-    def arrived(self, n):
-        self.settle(4, n, 4, 8, 4 * HALF)
-
-    def load(self, n, slot, gu_v, d_v, sem):
-        p = self.p
-        gu, d = gu_v.at[slot], d_v.at[slot]
+        to = self.p.at(dc=1)
+        full = self.gu.at[n], self.d.at[n]
+        self.own(n, kinds, [ref.at[0, c] for ref in full], lambda src, dst, i: send(src, dst, ss.at[i], rs.at[i], to))
+        for i in kinds:
+            ref = full[i].at[pl.ds(1, 3), c]
+            send(ref, ref, ss.at[i], rs.at[i], to)
+
+    def load(self, n, slot, into, sem, kinds=KINDS):
+        p = self.p
+        on(n < self.total)(lambda: self.settle(4, n, kinds, 4, 8, HALF))
+        n = lax.rem(n, self.total)
+        full = self.gu.at[n], self.d.at[n]
+        sizes = self.rows, HALF
+        place = lambda i, x, c: into[i].at[slot, rows_at((2 * x + c) * sizes[i], sizes[i], PART), :]
         start = lambda src, dst, i: pltpu.make_async_copy(src, dst, sem.at[slot, i]).start()
-        self.own(n, gu, d, start)
-        spans = [self.device_rows(p.x, 1 - p.c)]
-        for dx in OTHERS:
-            x = lax.rem(p.x + dx, RING)
-            spans.append((rows_at(2 * x * self.rows, 2 * self.rows, 8), rows_at(x * BLOCK, BLOCK)))
-        for gu_rows, d_rows in spans:
-            start(self.gu.at[n, gu_rows, :], gu.at[gu_rows, :], 0)
-            start(self.d.at[n, d_rows, :], d.at[d_rows, :], 1)
-
-    def loaded(self, slot, gu_v, d_v, sem):
-        drain(gu_v.at[slot], sem.at[slot, 0])
-        drain(d_v.at[slot], sem.at[slot, 1])
+        self.own(n, kinds, [place(i, p.x, p.c) for i in KINDS], start)
+        for i in kinds:
+            start(full[i].at[0, 1 - p.c], place(i, p.x, 1 - p.c), i)
+            for dx in OTHERS:
+                for c in range(2):
+                    start(full[i].at[dx, c], place(i, lax.rem(p.x + dx, RING), c), i)
 
 
 def vmem(*shape, dtype=bf16):
@@ -415,7 +402,7 @@
             drain(self.z.at[slot], self.c_r.at[q])
 
 
-def kernel(chunks, x_ref, dy_ref, wg, wu, wd, full_gu, full_d, lent, kept, h_ref, dx_ref, out_g, out_u, out_d, *scratch):
+def kernel(chunks, x_ref, dy_ref, wg, wu, wd, full_gu, full_d, lent, kept, h_ref, spill, dx_ref, out_g, out_u, out_d, *scratch):
     a_v, dy_v, da_v, gu_v, d_v, dgu_v, act_v, kept_v, own, (ss, rs, ld_sem, kept_sem, io_sem, lend_sem), reduces = scratch
     p = Place()
     meet([p.at(dc=1)] + [p.at(dx=side) for side in SIDES] + [p.at(**{axis: step}, dc=dc) for axis in ("dy", "dz") for step in OTHERS for dc in range(2)])
@@ -443,61 +430,39 @@
         a_v[t, :] = normed(dy_v[t, :])
         da_v[t, :] = jnp.zeros((small, d), f32)
 
+    into = (gu_v, d_v)
     tiles(0, 1, 4, first_norm)
     g.settle_lend(lend_sem)
     g.x1_down(0)
+    tiles(1, 3, 4, first_norm)
+    g.x2(0, WIDE)
+    g.x2(0, DOWN)
     g.x1(1)
-    tiles(1, 3, 4, first_norm)
-    g.x2(0)
     tiles(3, 4, 4, first_norm)
+    g.yz1(0, WIDE)
+    g.yz1(0, DOWN)
     g.x2(1)
-    g.settle_x2(0)
-    g.yz1(0)
-    g.settle_x2(1)
+    g.x1(2)
+    g.yz2(0, WIDE)
+    g.yz2(0, DOWN)
     g.yz1(1)
-    g.x1(2)
-    g.settle_yz1(0)
-    g.yz2(0)
+    g.x2(2)
     g.x1(3)
-    g.x2(2)
-    g.settle_yz2(0)
-    g.across(0)
-    g.settle_yz1(1)
+    g.across(0, WIDE)
+    g.across(0, DOWN)
+    g.yz1(2)
+    g.load(0, 0, into, ld_sem, WIDE)
+    g.load(0, 0, into, ld_sem, DOWN)
     g.yz2(1)
-    g.settle_x2(2)
-    g.yz1(2)
     g.x2(3)
-    g.arrived(0)
-    g.load(0, 0, gu_v, d_v, ld_sem)
+    g.x1(4)
+
+    def loaded(n, i):
+        drain(into[i].at[lax.rem(n, 2)], ld_sem.at[lax.rem(n, 2), i])
 
     def gather_on(n):
-        @on(n + 1 < total)
-        def _():
-            g.settle_yz2(n + 1)
-            g.across(n + 1)
-
-        @on(n + 2 < total)
-        def _():
-            g.settle_yz1(n + 2)
-            g.yz2(n + 2)
-
-        @on(n + 3 < total)
-        def _():
-            g.settle_x2(n + 3)
-            g.yz1(n + 3)
-
-        @on(n + 4 < total)
-        def _():
-            g.x1(n + 4)
-
-    def gather_more(n):
-        @on(n + 4 < total)
-        def _():
-            g.x2(n + 4)
-
-        @on(n + 1 < total)
-        def _():
-            g.arrived(n + 1)
+        for i, step in enumerate((g.across, g.yz2, g.yz1, g.x2, g.x1)):
+            on(n + i + 1 < total)(functools.partial(step, n + i + 1))
 
     def forward_part(k, i):
         slot = lax.rem(k, 2)
@@ -511,30 +476,36 @@
         pltpu.make_async_copy(kept_v.at[i], kept.at[k, t, :], kept_sem.at[i]).start()
         gate, up = kept_v[i, :, :CHUNK], kept_v[i, :, CHUNK:]
         act = (jax.nn.silu(gate) * up).astype(bf16)
+        on(i == 0)(lambda: loaded(k, 1))
         da_v[t, :] += dot(act, d_v[slot])
 
     @pl.loop(0, chunks)
     def _(k):
-        gather_on(k)
-        g.loaded(lax.rem(k, 2), gu_v, d_v, ld_sem)
-        forward_part(k, 0)
-        gather_more(k)
-        g.load(k + 1, lax.rem(k + 1, 2), gu_v, d_v, ld_sem)
-        forward_part(k, 1)
+        on(k > 0)(lambda: gather_on(k))
+        loaded(k, 0)
+
+        @pl.loop(0, 2)
+        def _(i):
+            @on(i == 1)
+            def _():
+                on(k == 0)(lambda: gather_on(k))
+                on(k > 0)(lambda: g.load(k + 1, lax.rem(k + 1, 2), into, ld_sem))
+
+            forward_part(k, i)
+
+        on(k == 0)(lambda: g.load(k + 1, lax.rem(k + 1, 2), into, ld_sem))
 
     def between(t):
         h = add_up(dy_v[t, :], da_v[t, :].astype(bf16))
+        dy_v[t, :] = h
         a_v[t, :] = normed(h)
         da_v[t, :] = jnp.zeros((small, d), f32)
-        dgu_v[t, :] = h[:, :BOTH]
-        act_v[t, : d - BOTH] = h[:, BOTH:]
-        pltpu.make_async_copy(dy_ref.at[t, :], dy_v.at[t, :], io_sem.at[0]).start()
-        pltpu.make_async_copy(dgu_v.at[t, :], h_ref.at[t, :BOTH], io_sem.at[1]).start()
-        pltpu.make_async_copy(act_v.at[t, : d - BOTH], h_ref.at[t, BOTH:], io_sem.at[1]).start()
+        pltpu.make_async_copy(dy_v.at[t, :], h_ref.at[t, :], io_sem.at[1]).start()
 
     tiles(0, 1, 1, between)
-    drain(dy_v, io_sem.at[0])
-    drain(a_v, io_sem.at[1])
+    drain(dy_v, io_sem.at[1])
+    dy_copy = pltpu.make_async_copy(dy_ref, dy_v, io_sem.at[0])
+    dy_copy.start()
     for i in range(2):
         drain(kept_v.at[i], kept_sem.at[i])
 
@@ -544,9 +515,6 @@
 
     def fetch(ref):
         return pltpu.make_async_copy(ref, a_v, io_sem.at[0])
-
-    def number(q):
-        return (1 - q // chunks) * chunks + lax.rem(q, chunks)
 
     def keep(t):
         b = lax.rem(t, 2)
@@ -584,6 +552,8 @@
             if joined:
                 da_tile(t, 1 - slot)
             gu = dot(a_v[t, :], gu_v[slot])
+            if not joined:
+                on(i == 0)(dy_copy.wait)
             through_gate(t, gu[:, :CHUNK], gu[:, CHUNK:], slot)
 
         def layer0(joined):
@@ -598,9 +568,16 @@
             def _():
                 keep(n + 2).start()
 
+        joins = (k > 0) & (q != total - 1)
         for joined in (False, True):
-            on((q < chunks) & ((k > 0) == joined))(functools.partial(layer1, joined))
-            on((q >= chunks) & (q < total) & ((k > 0) == joined))(functools.partial(layer0, joined))
+            on((q < chunks) & (joins == joined))(functools.partial(layer1, joined))
+            on((q >= chunks) & (q < total) & (joins == joined))(functools.partial(layer0, joined))
+
+    away_copy = pltpu.make_async_copy(dgu_v, spill, io_sem.at[1])
+
+    def back_copy(i):
+        t = rows_at(i * half, half)
+        return pltpu.make_async_copy(spill.at[t, :], dgu_v.at[t, :], kept_sem.at[i])
 
     @pl.loop(0, total + 4)
     def _(q):
@@ -619,11 +596,22 @@
         def _():
             each("yz2", q - 3)
 
-        @on((q == chunks) | (q == total))
-        def _():
-            @pl.loop(0, 2)
-            def _(i):
-                da_tile(rows_at(i * half, half), 1 - side)
+        @pl.loop(0, jnp.where(q == total, 4, jnp.where(q == chunks, 2, 0)))
+        def _(i):
+            j = lax.rem(i, 2)
+            on((q == total) & (i == 1))(lambda: each("x1", q - 1))
+
+            @on(i == 3)
+            def _():
+                each("yz3", q - 3)
+                each("yz1", q - 2)
+                each("x2", q - 1)
+
+            on(i >= 2)(back_copy(j).wait)
+            da_tile(rows_at(j * half, half), jnp.where(i < 2, 1 - side, side))
+            on((q == total) & (i < 2))(back_copy(j).start)
+
+        on(q == total - 1)(away_copy.wait)
 
         @on(q == chunks)
         def _():
@@ -644,29 +632,30 @@
 
         @on(busy)
         def _():
-            g.loaded(side, gu_v, d_v, ld_sem)
+            loaded(ahead, 0)
+            loaded(ahead, 1)
 
         @pl.loop(0, 2)
         def _(i):
-            @on(one & (i == 1))
+            @on((q >= 1) & (q < total) & (i == 1))
             def _():
                 each("x1", q - 1)
 
             gate_part(q, side, i)
 
-        @on(three)
+        on(q == total - 2)(away_copy.start)
+
+        @on(three & (q != total))
         def _():
             each("yz3", q - 3)
 
-        @on(two)
+        @on(two & (q != total))
         def _():
             each("yz1", q - 2)
 
-        gather_more(ahead)
-
         @on(q + 1 < total)
         def _():
-            g.load(number(q + 1), 1 - side, gu_v, d_v, ld_sem)
+            g.load(ahead + 1, 1 - side, into, ld_sem)
 
         @on(busy)
         def _():
@@ -678,7 +667,7 @@
             fetch(x_ref).wait()
             through_norm(0, 1, lambda t: None)
 
-        @on(one)
+        @on(one & (q != total))
         def _():
             each("x2", q - 1)
 
@@ -712,7 +701,7 @@
     tokens, d = x.shape
     layers, rows, _ = wg.shape
     n = layers * chunks
-    shapes = [(n, d, BOTH), (n, CHUNK, d), (layers, chunks // 2, HALF, d), (chunks, tokens, BOTH), x.shape, x.shape, wg.shape, wu.shape, wd.shape]
+    shapes = [(n, RING, 2, rows, BOTH), (n, RING, 2, HALF, d), (layers, chunks // 2, HALF, d), (chunks, tokens, BOTH), x.shape, (tokens, BOTH), x.shape, wg.shape, wu.shape, wd.shape]
     outs = [jax.ShapeDtypeStruct(shape, f32 if shape == (chunks, tokens, BOTH) else bf16) for shape in shapes]
     scratch = [vmem(tokens, d)] * 2 + [vmem(tokens, d, dtype=f32), vmem(2, d, BOTH), vmem(2, CHUNK, d)]
     scratch += [vmem(tokens, BOTH), vmem(tokens, CHUNK), vmem(2, tokens // 2, BOTH, dtype=f32)]
@@ -734,7 +723,7 @@
 
 def solution(mesh):
     def step(x, dy, wg, wu, wd):
-        dx, *out = call(x[0], dy[0], wg, wu, wd, wg.shape[2] // CHUNK)[5:]
+        dx, *out = call(x[0], dy[0], wg, wu, wd, wg.shape[2] // CHUNK)[6:]
         return dx[None], *out
 
     states, cut = P(("rep", "r", "s"), None, None), P(None, "s", None)

time: 574 us -> 569 us (level)
  no operation moved by 1% of the time
where the time goes in v3:
time: 569 us; the launch traced here: 568 us
  Pallas kernels  556 us (98%)
  local copies, waits for them, and re-layouts  12 us (2%)
    pallas_call x1, Pallas kernels, call(): pl.pallas_call(functools.partial(kernel, chunks), in_specs=[any_] * len(i...  556 us
    unnamed x10, local copies, waits for them, and re-layouts  12 us

profile of v3, /device:TPU:0, one launch (start us, length us, event | category | flops | bytes accessed | tf_op | source)
XLA Modules:
  0.0 568.3 jit_solution(2997224955981265638)
XLA Ops:
  0.6 555.7 %stack.1 = (bf16[18,4,2,144,1024]{4,3,2,1,0:T(8,128)(2,1)}, bf16[18,4,2,64,1152]{4,3,2,1,0:T(8,128)(2,1)}, bf16[2,4,64,1152]{3,2,1,0:T(8,128)(2,1)}, f32[9,2048,...) custom-call(bf16[2048,1152]{1,0:T(8,128)(2,1)} %bitcast.4, ...), custom_call_target="tpu_custom_call" | custom-call | tf_op jit(solution)/shard_map/stack/pallas_call | solution.py:713
  556.4 0.0 copy-start.2
  556.4 5.0 copy.13
  561.4 0.0 copy-done.2
  561.4 0.0 copy-start.1
  561.4 1.5 copy.14
  562.9 1.2 copy-done.1
  564.1 0.0 copy-start
  564.1 1.5 copy.15
  565.6 1.2 copy-done
  566.8 1.5 copy.16
Async XLA Ops:
  556.4 5.0 copy-start.2
  561.4 2.7 copy-start.1
  564.1 2.7 copy-start

commit v4 on v3

--- a/solution.py
+++ b/solution.py
@@ -588,13 +588,13 @@
         two = (q >= 2) & (q <= total + 1)
         three = (q >= 3) & (q <= total + 2)
 
+        @on(three & (q != total + 1))
+        def _():
+            each("yz2", q - 3)
+
         @on(q >= 4)
         def _():
             each("finish", q - 4)
-
-        @on(three)
-        def _():
-            each("yz2", q - 3)
 
         @pl.loop(0, jnp.where(q == total, 4, jnp.where(q == chunks, 2, 0)))
         def _(i):
@@ -666,6 +666,7 @@
         def _():
             fetch(x_ref).wait()
             through_norm(0, 1, lambda t: None)
+            each("yz2", q - 2)
 
         @on(one & (q != total))
         def _():
@@ -721,9 +722,42 @@
     )(*ins)
 
 
+def hand_on_kernel(cuts, *refs):
+    count = len(cuts)
+    ins, outs, bufs = (refs[i * count : (i + 1) * count] for i in range(3))
+    in_sem, out_sem = refs[3 * count :]
+    jobs = []
+    for src, dst, buf, cut in zip(ins, outs, bufs, cuts):
+        size = src.shape[0] // cut
+        for j in range(cut):
+            t = pl.ds(j * size, size)
+            i = len(jobs)
+            jobs.append((pltpu.make_async_copy(src.at[t], buf.at[t], in_sem.at[i]), pltpu.make_async_copy(buf.at[t], dst.at[t], out_sem.at[i])))
+    for come, _ in jobs:
+        come.start()
+    for come, go in jobs:
+        come.wait()
+        go.start()
+    for _, go in jobs:
+        go.wait()
+
+
+def hand_on(*arrays):
+    cuts = [8 if v.ndim == 2 else v.shape[0] for v in arrays]
+    any_ = pl.BlockSpec(memory_space=pl.ANY)
+    return pl.pallas_call(
+        functools.partial(hand_on_kernel, cuts),
+        in_specs=[any_] * len(arrays),
+        out_specs=[any_] * len(arrays),
+        out_shape=[jax.ShapeDtypeStruct(v.shape, bf16) for v in arrays],
+        scratch_shapes=[vmem(*v.shape) for v in arrays] + [dma(sum(cuts))] * 2,
+        name="hand_on",
+    )(*arrays)
+
+
 def solution(mesh):
     def step(x, dy, wg, wu, wd):
-        dx, *out = call(x[0], dy[0], wg, wu, wd, wg.shape[2] // CHUNK)[6:]
+        dx, *out = hand_on(*call(x[0], dy[0], wg, wu, wd, wg.shape[2] // CHUNK)[6:])
         return dx[None], *out
 
     states, cut = P(("rep", "r", "s"), None, None), P(None, "s", None)

time: 569 us -> 563 us (0.989)
  local copies, waits for them, and re-layouts: 12 us -> 0 us
  Pallas kernels: 556 us -> 562 us
    unnamed x10 -> x0, local copies, waits for them, and re-layouts: 12 us -> none
    pallas_call x0 -> x1, Pallas kernels: none -> 9.58 us  [hand_on(): pl.pallas_call(functools.partial(hand_on_kernel, cuts), in_specs=[any_] *...]
where the time goes in v4:
time: 563 us
  Pallas kernels  562 us (100%)
    pallas_call x1, Pallas kernels, call(): pl.pallas_call(functools.partial(kernel, chunks), in_specs=[any_] * len(i...  553 us

profile of v4, /device:TPU:0, one launch (start us, length us, event | category | flops | bytes accessed | tf_op | source)
XLA Modules:
  0.0 563.3 jit_solution(4729495492479699234)
XLA Ops:
  0.6 552.9 %stack.1 = (bf16[18,4,2,144,1024]{4,3,2,1,0:T(8,128)(2,1)}, bf16[18,4,2,64,1152]{4,3,2,1,0:T(8,128)(2,1)}, bf16[2,4,64,1152]{3,2,1,0:T(8,128)(2,1)}, f32[9,2048,...) custom-call(bf16[2048,1152]{1,0:T(8,128)(2,1)} %bitcast.3, ...), custom_call_target="tpu_custom_call" | custom-call | tf_op jit(solution)/shard_map/stack/pallas_call | solution.py:714
  553.5 9.6 %hand_on.1 = (bf16[2048,1152]{1,0:T(8,128)(2,1)}, bf16[2,144,4608]{2,1,0:T(8,128)(2,1)}, bf16[2,144,4608]{2,1,0:T(8,128)(2,1)}, bf16[2,576,1152]{2,1,0:T(8,128)(2,1)}) custom-call(bf16[2048,1152]{1,0:T(8,128)(2,1)} %get-tuple-element.12.refs_0_, bf16[2,144,4608]{2,1,0:T(8,128)(2,1)} %get-tuple-element.13.refs_1_, ...), custom_call_target="tpu_custom_call" | custom-call | tf_op jit(solution)/shard_map/hand_on/pallas_call | solution.py:748

commit v5 on v4

--- a/solution.py
+++ b/solution.py
@@ -617,16 +617,18 @@
         def _():
             fetch(h_ref).wait()
 
-            def then(t):
-                pltpu.make_async_copy(x_ref.at[t, :], a_v.at[t, :], io_sem.at[0]).start()
-
-            through_norm(0, 2, then)
-            fetch(x_ref).wait()
+            def then(t, sem):
+                pltpu.make_async_copy(x_ref.at[t, :], a_v.at[t, :], sem).start()
+
+            for i in range(2):
+                through_norm(i, i + 1, functools.partial(then, sem=io_sem.at[i]))
 
             def again(t):
                 a_v[t, :] = normed(a_v[t, :])
 
-            tiles(0, 1, 1, again)
+            for i in range(2):
+                drain(a_v.at[pl.ds(i * half, half), :], io_sem.at[i])
+                tiles(i, i + 1, 2, again)
 
         gather_on(ahead)
 
@@ -728,9 +730,9 @@
     in_sem, out_sem = refs[3 * count :]
     jobs = []
     for src, dst, buf, cut in zip(ins, outs, bufs, cuts):
-        size = src.shape[0] // cut
-        for j in range(cut):
-            t = pl.ds(j * size, size)
+        size = src.shape[-2] // cut
+        wholes = [(l,) for l in range(src.shape[0])] if len(src.shape) > 2 else [()]
+        for t in [(*whole, pl.ds(j * size, size)) for whole in wholes for j in range(cut)]:
             i = len(jobs)
             jobs.append((pltpu.make_async_copy(src.at[t], buf.at[t], in_sem.at[i]), pltpu.make_async_copy(buf.at[t], dst.at[t], out_sem.at[i])))
     for come, _ in jobs:
@@ -743,14 +745,15 @@
 
 
 def hand_on(*arrays):
-    cuts = [8 if v.ndim == 2 else v.shape[0] for v in arrays]
+    cuts = [8 if v.ndim == 2 else 3 for v in arrays]
+    pieces = sum(cut * (v.shape[0] if v.ndim > 2 else 1) for v, cut in zip(arrays, cuts))
     any_ = pl.BlockSpec(memory_space=pl.ANY)
     return pl.pallas_call(
         functools.partial(hand_on_kernel, cuts),
         in_specs=[any_] * len(arrays),
         out_specs=[any_] * len(arrays),
         out_shape=[jax.ShapeDtypeStruct(v.shape, bf16) for v in arrays],
-        scratch_shapes=[vmem(*v.shape) for v in arrays] + [dma(sum(cuts))] * 2,
+        scratch_shapes=[vmem(*v.shape) for v in arrays] + [dma(pieces)] * 2,
         name="hand_on",
     )(*arrays)
 

time: 563 us -> 563 us (level)
  no operation moved by 1% of the time
where the time goes in v5:
time: 563 us
  Pallas kernels  562 us (100%)
    pallas_call x1, Pallas kernels, call(): pl.pallas_call(functools.partial(kernel, chunks), in_specs=[any_] * len(i...  552 us

profile of v5, /device:TPU:0, one launch (start us, length us, event | category | flops | bytes accessed | tf_op | source)
XLA Modules:
  0.0 562.6 jit_solution(9147934935586077407)
XLA Ops:
  0.6 552.2 %stack.1 = (bf16[18,4,2,144,1024]{4,3,2,1,0:T(8,128)(2,1)}, bf16[18,4,2,64,1152]{4,3,2,1,0:T(8,128)(2,1)}, bf16[2,4,64,1152]{3,2,1,0:T(8,128)(2,1)}, f32[9,2048,...) custom-call(bf16[2048,1152]{1,0:T(8,128)(2,1)} %bitcast.3, ...), custom_call_target="tpu_custom_call" | custom-call | tf_op jit(solution)/shard_map/stack/pallas_call | solution.py:716
  552.8 9.6 %hand_on.1 = (bf16[2048,1152]{1,0:T(8,128)(2,1)}, bf16[2,144,4608]{2,1,0:T(8,128)(2,1)}, bf16[2,144,4608]{2,1,0:T(8,128)(2,1)}, bf16[2,576,1152]{2,1,0:T(8,128)(2,1)}) custom-call(bf16[2048,1152]{1,0:T(8,128)(2,1)} %get-tuple-element.12.refs_0_, bf16[2,144,4608]{2,1,0:T(8,128)(2,1)} %get-tuple-element.13.refs_1_, ...), custom_call_target="tpu_custom_call" | custom-call | tf_op jit(solution)/shard_map/hand_on/pallas_call | solution.py:751
